TPU v7x, 8 devices: a whole 2x2x1 slice. The times are simulated.
8 devices in a mesh: dp: 1 (over z), tp: 8 (over y, x, core).
Axes of the slice: x: 2, y: 2, z: 1, core: 2. Of those that a mesh axis runs over, the one named last changes fastest.
Arguments:
- x_in: bfloat16 [1, 128, 4096], P('dp', 'tp')
- start_pos: int32 [1], P('dp')
- k_cache: bfloat16 [1, 4096, 8, 128], P('dp', None, 'tp')
- v_cache: bfloat16 [1, 4096, 8, 128], P('dp', None, 'tp')
- attn_gain: bfloat16 [4096], replicated
- w_query: bfloat16 [4096, 32, 128], P(None, 'tp')
- w_key: bfloat16 [4096, 8, 128], P(None, 'tp')
- w_value: bfloat16 [4096, 8, 128], P(None, 'tp')
- w_out: bfloat16 [32, 128, 4096], P('tp')
- mlp_gain: bfloat16 [4096], replicated
- w_gate: bfloat16 [4096, 14336], P(None, 'tp')
- w_up: bfloat16 [4096, 14336], P(None, 'tp')
- w_down: bfloat16 [14336, 4096], P('tp')
Outputs:
- output 1: bfloat16 [1, 128, 4096], P('dp', 'tp')
- output 2: bfloat16 [1, 4096, 8, 128], P('dp', None, 'tp')
- output 3: bfloat16 [1, 4096, 8, 128], P('dp', None, 'tp')
All inputs are finite; a program needn't handle non-finite values.
Results may differ from a plain program's by a relative error of at most 0.0140087.
Values are sent between devices in bfloat16 or wider.
A program may use at most 1 GiB of HBM per device.

v0:
```python
import jax
import jax.numpy as jnp
from jax import lax
from jax.sharding import PartitionSpec as P

ROPE_BASE = 10000.0
NORM_EPS = 1e-5


def rms_norm(rows, gain):
    rows32 = rows.astype(jnp.float32)
    inv_rms = lax.rsqrt(jnp.mean(rows32 * rows32, axis=-1, keepdims=True) + NORM_EPS)
    return (rows32 * inv_rms * gain.astype(jnp.float32)).astype(jnp.bfloat16)


def rotate(heads_in, positions):
    head_dim = heads_in.shape[-1]
    inv_freq = jnp.power(ROPE_BASE, -jnp.arange(0, head_dim, 2).astype(jnp.float32) / head_dim)
    angles = positions.astype(jnp.float32)[..., None] * inv_freq
    lead = angles.shape[:2] + (1,) * (heads_in.ndim - 3) + (head_dim // 2,)
    cos_t = jnp.cos(angles).reshape(lead)
    sin_t = jnp.sin(angles).reshape(lead)
    pairs = heads_in.reshape(heads_in.shape[:-1] + (head_dim // 2, 2))
    even = pairs[..., 0]
    odd = pairs[..., 1]
    turned = jnp.stack([even * cos_t - odd * sin_t, even * sin_t + odd * cos_t], axis=-1)
    return turned.reshape(heads_in.shape)


def project_qkv(normed, positions, w_query, w_key, w_value):
    model_dim, kv_loc, head_dim = w_key.shape
    group = w_query.shape[1] // kv_loc
    w_query4 = w_query.reshape(model_dim, kv_loc, group, head_dim)
    q_lin = jnp.einsum('btd,dkge->btkge', normed, w_query4, preferred_element_type=jnp.float32)
    k_lin = jnp.einsum('btd,dke->btke', normed, w_key, preferred_element_type=jnp.float32)
    v_chunk = jnp.einsum('btd,dke->btke', normed, w_value, preferred_element_type=jnp.float32).astype(jnp.bfloat16)
    queries = rotate(q_lin, positions).astype(jnp.bfloat16)
    k_chunk = rotate(k_lin, positions).astype(jnp.bfloat16)
    return queries, k_chunk, v_chunk


def attend(queries, k_chunk, v_chunk, k_cache, v_cache, start_pos, tile_rows):
    rows, chunk_len, kv_loc, group, head_dim = queries.shape
    window = k_cache.shape[1]
    q_block = chunk_len
    while q_block > 8 and tile_rows * q_block > 256:
        q_block = q_block // 2
    n_blocks = chunk_len // q_block
    scale = head_dim ** -0.5
    offsets = jnp.mod(jnp.arange(window)[None, :] - start_pos[:, None], window)
    cache_valid = (start_pos[:, None] - window + offsets) >= 0
    key_ids = jnp.arange(chunk_len)

    def one_block(block):
        first = block * q_block
        q_tile = lax.dynamic_slice_in_dim(queries, first, q_block, axis=1)
        q_ids = first + jnp.arange(q_block)
        cache_mask = cache_valid[:, None, :] & (offsets[:, None, :] > q_ids[None, :, None])
        chunk_mask = key_ids[None, :] <= q_ids[:, None]
        s_cache = jnp.einsum('bqkge,bske->bkgqs', q_tile, k_cache, preferred_element_type=jnp.float32) * scale
        s_chunk = jnp.einsum('bqkge,bske->bkgqs', q_tile, k_chunk, preferred_element_type=jnp.float32) * scale
        s_cache = jnp.where(cache_mask[:, None, None], s_cache, -jnp.inf)
        s_chunk = jnp.where(chunk_mask, s_chunk, -jnp.inf)
        top = jnp.maximum(jnp.max(s_cache, axis=-1, keepdims=True), jnp.max(s_chunk, axis=-1, keepdims=True))
        e_cache = jnp.exp(s_cache - top)
        e_chunk = jnp.exp(s_chunk - top)
        total_mass = jnp.sum(e_cache, axis=-1, keepdims=True) + jnp.sum(e_chunk, axis=-1, keepdims=True)
        p_cache = (e_cache / total_mass).astype(jnp.bfloat16)
        p_chunk = (e_chunk / total_mass).astype(jnp.bfloat16)
        mixed = jnp.einsum('bkgqs,bske->bqkge', p_cache, v_cache, preferred_element_type=jnp.float32)
        mixed = mixed + jnp.einsum('bkgqs,bske->bqkge', p_chunk, v_chunk, preferred_element_type=jnp.float32)
        return mixed.astype(jnp.bfloat16)

    tiles = lax.map(one_block, jnp.arange(n_blocks))
    return tiles.reshape(n_blocks, rows, q_block, kv_loc * group, head_dim)


def write_chunk(cache, chunk, start_pos):
    window = cache.shape[1]
    chunk_len = chunk.shape[1]

    def one_row(old_rows, new_rows, start):
        filler = jnp.zeros((window - chunk_len,) + new_rows.shape[1:], new_rows.dtype)
        doubled = jnp.concatenate([new_rows, filler, new_rows, filler], axis=0)
        shift = jnp.mod(start, window)
        placed = lax.dynamic_slice_in_dim(doubled, window - shift, window, axis=0)
        offsets = jnp.mod(jnp.arange(window) - start, window)
        return jnp.where((offsets < chunk_len)[:, None, None], placed, old_rows)

    return jax.vmap(one_row)(cache, chunk, start_pos)


def swiglu(mlp_rows, w_gate, w_up):
    gate = jnp.einsum('btd,df->btf', mlp_rows, w_gate, preferred_element_type=jnp.float32)
    up_proj = jnp.einsum('btd,df->btf', mlp_rows, w_up, preferred_element_type=jnp.float32)
    return (jax.nn.silu(gate) * up_proj).astype(jnp.bfloat16)


def solution(mesh):
    row_spec = P('dp', 'tp', None)
    cache_spec = P('dp', None, 'tp', None)
    head_cols = P(None, 'tp', None)
    in_specs = (row_spec, P('dp'), cache_spec, cache_spec, P(), head_cols, head_cols, head_cols, P('tp', None, None), P(), P(None, 'tp'), P(None, 'tp'), P('tp', None))
    out_specs = (row_spec, cache_spec, cache_spec)

    def local_layer(x_in, start_pos, k_cache, v_cache, attn_gain, w_query, w_key, w_value, w_out, mlp_gain, w_gate, w_up, w_down):
        rows = x_in.shape[0]
        model_dim = x_in.shape[2]
        attn_rows = lax.all_gather(rms_norm(x_in, attn_gain), 'tp', axis=1, tiled=True)
        chunk_len = attn_rows.shape[1]
        positions = start_pos[:, None] + jnp.arange(chunk_len)[None, :]
        queries, k_chunk, v_chunk = project_qkv(attn_rows, positions, w_query, w_key, w_value)
        mixed = attend(queries, k_chunk, v_chunk, k_cache, v_cache, start_pos, rows)
        attn_part = jnp.einsum('nbqhe,hed->bnqd', mixed, w_out, preferred_element_type=jnp.float32)
        attn_part = attn_part.reshape(rows, chunk_len, model_dim).astype(jnp.bfloat16)
        attn_sum = lax.psum_scatter(attn_part, 'tp', scatter_dimension=1, tiled=True)
        hidden = (x_in.astype(jnp.float32) + attn_sum.astype(jnp.float32)).astype(jnp.bfloat16)
        mlp_rows = lax.all_gather(rms_norm(hidden, mlp_gain), 'tp', axis=1, tiled=True)
        activated = swiglu(mlp_rows, w_gate, w_up)
        mlp_part = jnp.einsum('btf,fd->btd', activated, w_down, preferred_element_type=jnp.float32).astype(jnp.bfloat16)
        mlp_sum = lax.psum_scatter(mlp_part, 'tp', scatter_dimension=1, tiled=True)
        x_out = (hidden.astype(jnp.float32) + mlp_sum.astype(jnp.float32)).astype(jnp.bfloat16)
        return x_out, write_chunk(k_cache, k_chunk, start_pos), write_chunk(v_cache, v_chunk, start_pos)

    return jax.shard_map(local_layer, mesh=mesh, in_specs=in_specs, out_specs=out_specs, check_vma=False)
```

profile of v0, /device:TPU:0, one launch (start us, length us, event | category | flops | bytes accessed | tf_op | source)
XLA Modules:
  0.0 158.4 jit_solution(17153959868815724132)
XLA Ops:
  7.2 0.8 convert_element_type.149
  8.0 1.0 fusion.42
  9.1 1.7 %fusion.44 = bf16[1,16,4096]{2,1,0:T(8,128)(2,1)} fusion(bf16[1,16,4096]{2,1,0:T(8,128)(2,1)} %param.13, f32[4096]{0:T(1024)S(1)} %convert_element_type.149, f32[16]{0:T(128)S(1)} %add_rsqrt_fusion.1), kind=kLoop, calls=%fused_computation.61 | loop fusion | flops 262144 | bytes 278592 | tf_op jit(solution)/shard_map/convert_element_type | solution.py:13
  11.5 9.6 %copy.27 = bf16[4,128,4096]{2,0,1:T(4,128)(2,1)} copy(bf16[4,128,4096]{1,0,2:T(4,128)(2,1)} %bitcast.171) | data formatting | bytes 8388608 | tf_op jit(solution)/shard_map/btd,dkge->btkge/dot_general | solution.py:34
  21.0 0.5 copy.36
  21.6 1.5 reshape.606
  23.3 0.4 fusion.9
  23.7 7.6 %all-gather.3.cloned.1.call-done = bf16[1,128,4096]{2,1,0:T(8,128)(2,1)} async-done(((bf16[1,16,4096]{2,1,0:T(8,128)(2,1)}), bf16[1,128,4096]{2,1,0:T(8,128)(2,1)}) %all-gather.3.cloned.1.call-update) | async-done | bytes 1048592 | tf_op jit(solution)/shard_map/all_gather | solution.py:109
  31.3 7.2 %fusion.14 = f32[1,128,1,4,64,2]{1,4,5,3,2,0:T(8,128)S(1)} fusion(bf16[4,64,2,4096]{3,0,2,1:T(4,128)(2,1)} %bitcast.172, bf16[1,128,4096]{2,1,0:T(8,128)(2,1)} %all-gather.3.cloned.1.call-done), kind=kOutput, calls=%fused_computation.27 | convolution fusion | flops 536870912 | bytes 5505024 | tf_op jit(solution)/shard_map/btd,dkge->btkge/dot_general | solution.py:34
  38.7 1.3 convolution_bitcast_fusion.2
  40.4 1.8 %fusion.82 = (f32[4,128]{1,0:T(4,128)S(1)}, f32[1,1,4,128,4096]{4,3,2,1,0:T(8,128)S(1)}) fusion(bf16[128,4,128]{0,2,1:T(8,128)(2,1)S(1)} %bitcast.174, bf16[1,4096,1,128]{3,1,2,0:T(8,128)(2,1)S(1)} %copy-done.3, pred[128,4096]{1,0:T(8,128)(4,1)S(1)} %fusion.9), kind=kOutput, calls=%fused_computation.117 | convolution fusion | flops 543161856 | bytes 10094592 | tf_op jit(solution)/shard_map/while/body/eval_jaxpr/bqkge,bske->bkgqs/dot_general | solution.py:60
  42.5 1.3 fusion
  43.8 2.3 %fusion.17 = f32[128,4,128]{0,2,1:T(8,128)S(1)} fusion(f32[4,128]{1,0:T(4,128)S(1)} %add.154, f32[1,1,4,128,4096]{4,3,2,1,0:T(8,128)S(1)} %get-tuple-element.62, f32[4,128]{1,0:T(4,128)S(1)} %max.9, bf16[1,4096,1,128]{3,1,2,0:T(8,128)(2,1)S(1)} %copy-done.9), kind=kOutput, calls=%fused_computation.30 | convolution fusion | flops 543162368 | bytes 9703424 | tf_op jit(solution)/shard_map/while/body/eval_jaxpr/bkgqs,bske->bqkge/dot_general | solution.py:70
  46.1 0.4 convolution_convert_fusion.1
  46.6 4.1 %fusion.2 = bf16[1,128,4096]{2,1,0:T(8,128)(2,1)} fusion(bf16[4,128,4096]{2,1,0:T(8,128)(2,1)} %param.21, f32[128,4,128]{0,2,1:T(8,128)S(1)} %fusion.17, f32[1,1,4,128,128]{3,4,2,1,0:T(8,128)S(1)} %get-tuple-element.64, f32[4,128]{1,0:T(4,128)S(1)} %add.154, f32[4,128]{1,0:T(4,128)S(1)} %max.9, bf16[128,128]{1,0:T(8,128)(2,1)S(1)} %convolution_convert_fusion.1), kind=kOutput, calls=%fused_computation.7 | convolution fusion | flops 554500096 | bytes 5804032 | tf_op jit(solution)/shard_map/nbqhe,hed->bnqd/dot_general | solution.py:114
  50.8 27.6 %reduce-scatter.3.cloned.1.call-done = bf16[1,16,4096]{2,1,0:T(8,128)(2,1)} async-done(((bf16[1,128,4096]{2,1,0:T(8,128)(2,1)}), bf16[1,16,4096]{2,1,0:T(8,128)(2,1)}) %reduce-scatter.3.cloned.1.call-update) | async-done | bytes 131088 | tf_op jit(solution)/shard_map/reduce_scatter | solution.py:116
  78.4 1.1 fusion.46
  79.5 1.7 %fusion.48 = bf16[1,16,4096]{2,1,0:T(8,128)(2,1)} fusion(f32[4096]{0:T(1024)S(1)} %convert_element_type.168, f32[16]{0:T(128)S(1)} %add_rsqrt_fusion, bf16[1,16,4096]{2,1,0:T(8,128)(2,1)} %reduce-scatter.3.cloned.1.call-done, bf16[1,16,4096]{2,1,0:T(8,128)(2,1)S(1)} %copy-done.4), kind=kLoop, calls=%fused_computation.65 | loop fusion | flops 524288 | bytes 409664 | tf_op jit(solution)/shard_map/convert_element_type | solution.py:13
  81.2 17.7 %all-gather.5.cloned.1.call-done = bf16[1,128,4096]{2,1,0:T(8,128)(2,1)} async-done(((bf16[1,16,4096]{2,1,0:T(8,128)(2,1)}), bf16[1,128,4096]{2,1,0:T(8,128)(2,1)}) %all-gather.5.cloned.1.call-update) | async-done | bytes 1048592 | tf_op jit(solution)/shard_map/all_gather | solution.py:118
  98.9 8.6 %fusion.33 = f32[128,1792]{1,0:T(8,128)} fusion(bf16[4096,1792]{1,0:T(8,128)(2,1)} %param.23, bf16[1,128,4096]{2,1,0:T(8,128)(2,1)} %all-gather.5.cloned.1.call-done), kind=kOutput, calls=%fused_computation.46 | convolution fusion | flops 1879048192 | bytes 16646144 | tf_op jit(solution)/shard_map/btd,df->btf/dot_general | solution.py:94
  107.4 15.1 %fusion.3 = bf16[1,128,4096]{2,1,0:T(8,128)(2,1)} fusion(bf16[1792,4096]{1,0:T(8,128)(2,1)} %param.25, bf16[4096,1792]{1,0:T(8,128)(2,1)} %param.24, bf16[1,128,4096]{2,1,0:T(8,128)(2,1)S(1)} %copy-done.2, f32[128,1792]{1,0:T(8,128)} %fusion.33), kind=kOutput, calls=%fused_computation.8 | convolution fusion | flops 3759996928 | bytes 32374784 | tf_op jit(solution)/shard_map/btf,fd->btd/dot_general | solution.py:120
  122.9 8.5 %fusion.26 = (bf16[1,4096,1,128]{3,1,2,0:T(8,128)(2,1)}, bf16[1,4096,1,128]{3,1,2,0:T(8,128)(2,1)}) fusion(bf16[1,4096,1,128]{3,1,2,0:T(8,128)(2,1)} %param.16, s32[]{:T(128)} %bitcast.49, bf16[1,3968,1,128]{3,1,2,0:T(8,128)(2,1)S(1)} %broadcast.426, bf16[1,128,1,128]{3,1,2,0:T(8,128)(2,1)S(1)} %bitcast.175, pred[4096]{0:T(1024)(128)(4,1)S(1)} %broadcast_compare_fusion, ...), kind=kLoop, calls=%fused_computation.39 | loop fusion | flops 9437184 | bytes 5279748 | tf_op jit(solution)/shard_map/vmap(jit(_where))/select_n | solution.py:88
  131.4 18.8 %reduce-scatter.5.cloned.1.call-done = bf16[1,16,4096]{2,1,0:T(8,128)(2,1)} async-done(((bf16[1,128,4096]{2,1,0:T(8,128)(2,1)}), bf16[1,16,4096]{2,1,0:T(8,128)(2,1)}) %reduce-scatter.5.cloned.1.call-update) | async-done | bytes 131088 | tf_op jit(solution)/shard_map/reduce_scatter | solution.py:121
  150.3 1.6 %fusion.49 = bf16[1,16,4096]{2,1,0:T(8,128)(2,1)} fusion(bf16[1,16,4096]{2,1,0:T(8,128)(2,1)} %reduce-scatter.5.cloned.1.call-done, bf16[1,16,4096]{2,1,0:T(8,128)(2,1)S(1)} %copy-done.5, bf16[1,16,4096]{2,1,0:T(8,128)(2,1)S(1)} %copy-done.4), kind=kLoop, calls=%fused_computation.66 | loop fusion | flops 524288 | bytes 524288 | tf_op jit(solution)/shard_map/convert_element_type | solution.py:122
  (55 shorter events, 1.7 us)
Async XLA Ops:
  7.2 38.9 %copy-start = (bf16[4096,1,128]{2,0,1:T(8,128)(2,1)S(1)}, bf16[4096,1,128]{2,0,1:T(8,128)(2,1)}, u32[]{:S(2)}) copy-start(bf16[4096,1,128]{2,0,1:T(8,128)(2,1)} %param.20) | copy-start | bytes 3145732
  7.2 24.1 %all-gather.3.cloned.1.call-start = ((), (), s32[]{:S(2)}) async-start(), calls=%async_computation.2 | async-start | bytes 1179648 | tf_op jit(solution)/shard_map/all_gather | solution.py:109
  10.8 67.6 %reduce-scatter.3.cloned.1.call-start = ((), (), s32[]{:S(2)}) async-start(), calls=%async_computation.3 | async-start | bytes 1179648 | tf_op jit(solution)/shard_map/reduce_scatter | solution.py:116
  11.5 9.6 %copy-start.6 = (bf16[4096,1,128]{2,0,1:T(8,128)(2,1)S(1)}, bf16[4096,1,128]{2,0,1:T(8,128)(2,1)}, u32[]{:S(2)}) copy-start(bf16[4096,1,128]{2,0,1:T(8,128)(2,1)} %param.19) | copy-start | bytes 3145732
  31.3 7.4 %copy-start.7 = (bf16[1,128,4096]{2,1,0:T(8,128)(2,1)S(1)}, bf16[1,128,4096]{2,1,0:T(8,128)(2,1)}, u32[]{:S(2)}) copy-start(bf16[1,128,4096]{2,1,0:T(8,128)(2,1)} %all-gather.3.cloned.1.call-done) | copy-start | bytes 3145732
  31.3 7.4 %copy-start.8 = (bf16[64,2,4096]{2,1,0:T(2,128)(2,1)S(1)}, bf16[64,2,4096]{2,1,0:T(2,128)(2,1)}, u32[]{:S(2)}) copy-start(bf16[64,2,4096]{2,1,0:T(2,128)(2,1)} %reshape.606) | copy-start | bytes 3145732
  31.3 9.1 %copy-start.3 = (bf16[1,4096,1,128]{3,1,2,0:T(8,128)(2,1)S(1)}, bf16[1,4096,1,128]{3,1,2,0:T(8,128)(2,1)}, u32[]{:S(2)}) copy-start(bf16[1,4096,1,128]{3,1,2,0:T(8,128)(2,1)} %param.15) | copy-start | bytes 3145732
  42.5 1.3 copy-start.9
  46.1 4.6 %copy-start.10 = (bf16[4096]{0:T(1024)(128)(2,1)S(1)}, bf16[4096]{0:T(1024)(128)(2,1)}, u32[]{:S(2)}) copy-start(bf16[4096]{0:T(1024)(128)(2,1)} %param.22) | copy-start | bytes 24580
  46.1 32.3 %copy-start.4 = (bf16[1,16,4096]{2,1,0:T(8,128)(2,1)S(1)}, bf16[1,16,4096]{2,1,0:T(8,128)(2,1)}, u32[]{:S(2)}) copy-start(bf16[1,16,4096]{2,1,0:T(8,128)(2,1)} %param.13) | copy-start | bytes 393220
  50.7 48.2 %all-gather.5.cloned.1.call-start = ((), (), s32[]{:S(2)}) async-start(), calls=%async_computation.4 | async-start | bytes 1179648 | tf_op jit(solution)/shard_map/all_gather | solution.py:118
  81.1 69.1 %reduce-scatter.5.cloned.1.call-start = ((), (), s32[]{:S(2)}) async-start(), calls=%async_computation.5 | async-start | bytes 1179648 | tf_op jit(solution)/shard_map/reduce_scatter | solution.py:121
  98.9 8.6 %copy-start.2 = (bf16[1,128,4096]{2,1,0:T(8,128)(2,1)S(1)}, bf16[1,128,4096]{2,1,0:T(8,128)(2,1)}, u32[]{:S(2)}) copy-start(bf16[1,128,4096]{2,1,0:T(8,128)(2,1)} %all-gather.5.cloned.1.call-done) | copy-start | bytes 3145732
  107.4 44.4 %copy-start.1 = (bf16[4096,1,128]{2,0,1:T(8,128)(2,1)S(1)}, bf16[4096,1,128]{2,0,1:T(8,128)(2,1)}, u32[]{:S(2)}) copy-start(bf16[4096,1,128]{2,0,1:T(8,128)(2,1)} %param.20) | copy-start | bytes 3145732
  122.5 27.7 %copy-start.5 = (bf16[1,16,4096]{2,1,0:T(8,128)(2,1)S(1)}, bf16[1,16,4096]{2,1,0:T(8,128)(2,1)}, u32[]{:S(2)}) copy-start(bf16[1,16,4096]{2,1,0:T(8,128)(2,1)} %reduce-scatter.3.cloned.1.call-done) | copy-start | bytes 393220
Sparse Core Ops, SparseCore 0:
  10.9 20.3 all-gather.2
  50.8 27.5 reduce-scatter.2
  81.3 17.5 all-gather.4
  122.7 27.5 reduce-scatter.4
where the time goes:
time: 159 us; the launch traced here: 158 us
  waiting for transfers between devices  71.8 us (45%)
  matrix products  41 us (26%)
  other arithmetic  18.7 us (12%)
  between operations  14.7 us (9%)
  local copies, waits for them, and re-layouts  12.1 us (8%)
    reduce_scatter x1, waiting for transfers between devices, local_layer(): lax.psum_scatter(attn_part, 'tp', scatter_dimension=1, tiled=True)  27.6 us
    reduce_scatter x1, waiting for transfers between devices, local_layer(): mlp_sum = lax.psum_scatter(mlp_part, 'tp', scatter_dimension=1, tiled=True)  18.8 us
    all_gather x1, waiting for transfers between devices, local_layer(): lax.all_gather(rms_norm(hidden, mlp_gain), 'tp', axis=1, tiled=True)  17.7 us
    dot_general x1, matrix products, local_layer(): jnp.einsum('btf,fd->btd', activated, w_down, preferred_element_type=jnp.f...  15.1 us
    dot_general x1, local copies, waits for them, and re-layouts, project_qkv(): jnp.einsum('btd,dkge->btkge', normed, w_query4, preferred_element_type=jn...  9.56 us
    dot_general x1, matrix products, swiglu(): jnp.einsum('btd,df->btf', mlp_rows, w_gate, preferred_element_type=jnp.fl...  8.57 us
    select_n x1, other arithmetic, one_row(): return jnp.where((offsets < chunk_len)[:, None, None], placed, old_rows)  8.52 us
    all_gather x1, waiting for transfers between devices, local_layer(): lax.all_gather(rms_norm(x_in, attn_gain), 'tp', axis=1, tiled=True)  7.59 us
  transfers between devices with their start and end apart: 4, of which 4 were waited for; matrix products, arithmetic and copies ran while one was open for 13% of the time, Pallas kernels for 0%

commit v1 on v0

v1 whole, which is shorter than its diff:
```python
import functools

import jax
import jax.numpy as jnp
from jax import lax
from jax.experimental import pallas as pl
from jax.experimental.pallas import tpu as pltpu
from jax.sharding import PartitionSpec as P

ROPE_BASE = 10000.0
NORM_EPS = 1e-5
BF16 = jnp.bfloat16
F32 = jnp.float32
D = 4096
T = 128
FF = 1792
W = 4096
NP = 4
CW = D // NP
KB = 512
NKB = W // KB


def token_of_row(row):
    core = row // 64
    chip = (row // 16) % 4
    return 32 * chip + 16 * core + row % 16


def layer_kernel(start_ref, x_hbm, cos_hbm, sin_hbm, kc_hbm, vc_hbm, g1_hbm, wq_hbm, wk_hbm, wv_hbm, wo_hbm, g2_hbm, wg_hbm, wu_hbm, wd_hbm,
                 xo_ref, kch_ref, vch_ref,
                 xv, g1, g2, wg, wu, xg1, xg2, pbuf, ra, sb, rb, hb,
                 lsem, wsem, dsem, send_sem, recv_sem, fsend_sem, frecv_sem, asend_sem, arecv_sem, bsend_sem, brecv_sem):
    me = lax.axis_index("tp")
    core = me % 2
    chip = me // 2
    other = 1 - core
    partner = 2 * chip + other
    flip1 = chip + 1 - 2 * (chip % 2)
    flip2 = chip + 2 - 4 * (chip // 2)
    flip3 = 3 - chip
    chips = (chip, flip1, flip2, flip3)
    my_rows = pl.ds(pl.multiple_of(64 * core + 16 * chip, 16), 16)

    def rows_of(c, q):
        return pl.ds(pl.multiple_of(64 * c + 16 * q, 16), 16)

    def remote(src, dst, ssem, rsem, dev):
        return pltpu.make_async_remote_copy(src_ref=src, dst_ref=dst, send_sem=ssem, recv_sem=rsem, device_id={"tp": dev}, device_id_type=pl.DeviceIdType.MESH)

    def local(src, dst, sem):
        return pltpu.make_async_copy(src, dst, sem)

    def ag_direct(ph, xg, r, p):
        cols = pl.ds(p * CW, CW)
        return remote(xg.at[my_rows, cols], xg.at[my_rows, cols], send_sem.at[ph, r, p], recv_sem.at[ph, r, p], 2 * chips[r] + core)

    def ag_direct_in(ph, xg, r, p):
        ref = xg.at[rows_of(core, chips[r]), pl.ds(p * CW, CW)]
        return remote(ref, ref, send_sem.at[ph, r, p], recv_sem.at[ph, r, p], 2 * chips[r] + core)

    def ag_forward(ph, xg, r, p):
        ref = xg.at[rows_of(core, chips[r]), pl.ds(p * CW, CW)]
        return remote(ref, ref, fsend_sem.at[ph, r, p], frecv_sem.at[ph, r, p], partner)

    def ag_forward_in(ph, xg, r, p):
        ref = xg.at[rows_of(other, chips[r]), pl.ds(p * CW, CW)]
        return remote(ref, ref, fsend_sem.at[ph, r, p], frecv_sem.at[ph, r, p], partner)

    def ag_start(ph, xg):
        for p in range(NP):
            for r in (3, 1, 2):
                ag_direct(ph, xg, r, p).start()
            ag_forward(ph, xg, 0, p).start()

    def ag_relay(ph, xg, p):
        for r in (1, 2, 3):
            ag_direct_in(ph, xg, r, p).wait_recv()
            ag_forward(ph, xg, r, p).start()

    def ag_arrive(ph, xg, p):
        for r in (0, 1, 2, 3):
            ag_forward_in(ph, xg, r, p).wait_recv()

    def ag_finish(ph, xg):
        for p in range(NP):
            for r in (1, 2, 3):
                ag_direct(ph, xg, r, p).wait_send()
            for r in (0, 1, 2, 3):
                ag_forward(ph, xg, r, p).wait_send()

    def rs_a(ph, n):
        return remote(pbuf.at[ph, n, pl.ds(pl.multiple_of(64 * other, 64), 64), :], ra.at[ph, n], asend_sem.at[ph, n], arecv_sem.at[ph, n], partner)

    def rs_b(ph, n, r):
        return remote(sb.at[ph, n, pl.ds(pl.multiple_of(16 * chips[r], 16), 16), :], rb.at[ph, r - 1, n], bsend_sem.at[ph, r, n], brecv_sem.at[ph, r, n], 2 * chips[r] + core)

    def rs_put(ph, n, part):
        pbuf[ph, n] = part.astype(BF16)
        rs_a(ph, n).start()

    def rs_pair(ph, n):
        rs_a(ph, n).wait_recv()
        own = pbuf[ph, n, pl.ds(pl.multiple_of(64 * core, 64), 64), :].astype(F32)
        sb[ph, n] = (own + ra[ph, n].astype(F32)).astype(BF16)
        for r in (3, 1, 2):
            rs_b(ph, n, r).start()

    def rs_sum(ph, n):
        total = sb[ph, n, pl.ds(pl.multiple_of(16 * chip, 16), 16), :].astype(F32)
        for r in (1, 2, 3):
            rs_b(ph, n, r).wait_recv()
            total = total + rb[ph, r - 1, n].astype(F32)
        return total

    def rs_finish(ph):
        for n in range(NP):
            rs_a(ph, n).wait_send()
            for r in (1, 2, 3):
                rs_b(ph, n, r).wait_send()

    def normed(rows, gain):
        ms = jnp.zeros((16, 128), F32)
        for j in range(32):
            v = rows[:, 128 * j:128 * j + 128].astype(F32)
            ms = ms + v * v
        inv = lax.rsqrt(jnp.sum(ms, axis=-1, keepdims=True) * (1.0 / D) + NORM_EPS)
        return inv

    def store_normed(src, gain, dst):
        inv = normed(src, gain)
        for j in range(32):
            cols = slice(128 * j, 128 * j + 128)
            val = src[:, cols].astype(F32) * inv * gain[j:j + 1, :].astype(F32)
            dst[my_rows, cols] = val.astype(BF16)

    gate_loads = []
    for p in range(NP):
        gate_loads.append(local(wg_hbm.at[pl.ds(p * CW, CW), :], wg.at[pl.ds(p * CW, CW), :], wsem.at[0, p]))
        gate_loads.append(local(wu_hbm.at[pl.ds(p * CW, CW), :], wu.at[pl.ds(p * CW, CW), :], wsem.at[1, p]))

    def attention_phase(wq4, wqkv, kc, vc, vt, wo, cosv, sinv, qs, kch, vch, s_buf, o_buf):
        loads = {
            "x": local(x_hbm, xv, lsem.at[0]),
            "g1": local(g1_hbm, g1, lsem.at[1]),
            "wk": local(wk_hbm, wqkv.at[:, pl.ds(512, 128)], lsem.at[2]),
            "wv": local(wv_hbm, wqkv.at[:, pl.ds(640, 128)], lsem.at[3]),
            "vc": local(vc_hbm, vc, lsem.at[4]),
            "kc": local(kc_hbm, kc, lsem.at[5]),
            "cos": local(cos_hbm, cosv, lsem.at[6]),
            "sin": local(sin_hbm, sinv, lsem.at[7]),
            "wo": local(wo_hbm, wo, lsem.at[8]),
            "g2": local(g2_hbm, g2, lsem.at[9]),
        }
        loads["x"].start()
        loads["g1"].start()
        wq_loads = [local(wq_hbm.at[pl.ds(p * 4 * CW, 4 * CW), :], wq4.at[pl.ds(p * 4 * CW, 4 * CW), :], dsem.at[p]) for p in range(NP)]
        for ld in wq_loads:
            ld.start()
        for name in ("vc", "wk", "wv", "cos", "sin", "kc", "wo", "g2"):
            loads[name].start()

        barrier = pltpu.get_barrier_semaphore()
        for dev in (partner, 2 * flip1 + core, 2 * flip2 + core, 2 * flip3 + core):
            pl.semaphore_signal(barrier, inc=1, device_id={"tp": dev}, device_id_type=pl.DeviceIdType.MESH)

        loads["x"].wait()
        loads["g1"].wait()
        store_normed(xv, g1, xg1)
        pl.semaphore_wait(barrier, 4)
        ag_start(0, xg1)

        ri = lax.broadcasted_iota(jnp.int32, (256, 256), 0)
        ci = lax.broadcasted_iota(jnp.int32, (256, 256), 1)
        perm = (ci == 4 * (ri % 64) + ri // 64).astype(F32).astype(BF16)

        def split_heads(p):
            wq_loads[p].wait()

            def body(i, carry):
                base = p * (CW // 64) + i
                rows4 = wq4[pl.ds(pl.multiple_of(base * 256, 256), 256), :]
                out = jnp.dot(perm, rows4, preferred_element_type=F32).astype(BF16)
                for h in range(4):
                    wqkv[pl.ds(pl.multiple_of(base * 64, 64), 64), h * 128:h * 128 + 128] = out[64 * h:64 * h + 64, :]
                return carry

            lax.fori_loop(0, CW // 64, body, 0, unroll=4)

        split_heads(0)
        loads["vc"].wait()

        def flip_values(i, carry):
            ks = pl.ds(pl.multiple_of(i * KB, KB), KB)
            vt[:, ks] = vc[ks, :].astype(F32).T.astype(BF16)
            return carry

        lax.fori_loop(0, NKB, flip_values, 0)
        loads["wk"].wait()
        loads["wv"].wait()
        ag_relay(0, xg1, 0)
        acc = jnp.zeros((T, 768), F32)
        for p in range(NP):
            if p + 1 < NP:
                split_heads(p + 1)
            ag_arrive(0, xg1, p)
            cols = slice(p * CW, p * CW + CW)
            acc = acc + jnp.dot(xg1[:, cols], wqkv[cols, :], preferred_element_type=F32)
            if p + 1 < NP:
                ag_relay(0, xg1, p + 1)
        for ld in gate_loads:
            ld.start()
        loads["cos"].wait()
        loads["sin"].wait()

        lane = lax.broadcasted_iota(jnp.int32, (T, 128), 1)
        even = lane % 2 == 0
        cos_t = cosv[...]
        sin_t = sinv[...]

        def rotate(v):
            swapped = jnp.where(even, pltpu.roll(v, 127, 1), pltpu.roll(v, 1, 1))
            return v * cos_t + swapped * sin_t

        for h in range(4):
            qs[h * 128:h * 128 + 128, :] = rotate(acc[:, h * 128:h * 128 + 128]).astype(BF16)
        kch[...] = rotate(acc[:, 512:640]).astype(BF16)
        v_f32 = acc[:, 640:768]
        vch[...] = v_f32.astype(BF16)
        kch_ref[...] = kch[...]
        vch_ref[...] = vch[...]
        vt[:, W:W + T] = vch[...].astype(F32).T.astype(BF16)
        loads["kc"].wait()

        start = start_ref[0]
        tok_lane = token_of_row(lax.broadcasted_iota(jnp.int32, (1, 128), 1))
        factor = (128.0 ** -0.5) * 1.4426950408889634

        def half(hp, carry0):
            q2 = qs[pl.ds(pl.multiple_of(hp * 256, 256), 256), :]

            def scores(i, top):
                ks = pl.ds(pl.multiple_of(i * KB, KB), KB)
                st = lax.dot_general(kc[ks, :], q2, (((1,), (1,)), ((), ())), preferred_element_type=F32)
                slot = i * KB + lax.broadcasted_iota(jnp.int32, (KB, 128), 0)
                off = jnp.bitwise_and(slot - start, W - 1)
                thr = jnp.where(off >= W - start, off, -1)
                keep = thr > tok_lane
                for g in range(2):
                    part = jnp.where(keep, st[:, g * 128:g * 128 + 128], -jnp.inf)
                    s_buf[ks, g * 128:g * 128 + 128] = part
                    new = jnp.max(part.reshape(KB // 8, 8, 128), axis=0)
                    top = top[:g] + (jnp.maximum(top[g], new),) + top[g + 1:]
                return top

            st = lax.dot_general(kch[...], q2, (((1,), (1,)), ((), ())), preferred_element_type=F32)
            key_tok = token_of_row(lax.broadcasted_iota(jnp.int32, (T, 128), 0))
            keep = key_tok <= tok_lane
            top = ()
            for g in range(2):
                part = jnp.where(keep, st[:, g * 128:g * 128 + 128], -jnp.inf)
                s_buf[W:W + T, g * 128:g * 128 + 128] = part
                top = top + (jnp.max(part.reshape(T // 8, 8, 128), axis=0),)
            top = lax.fori_loop(0, NKB, scores, top)
            tops = tuple(jnp.max(t, axis=0, keepdims=True) for t in top)

            def expo(rows, n, mass):
                for g in range(2):
                    e = jnp.exp2((s_buf[rows, g * 128:g * 128 + 128] - tops[g]) * factor)
                    s_buf[rows, g * 128:g * 128 + 128] = e
                    mass = mass[:g] + (mass[g] + jnp.sum(e.reshape(n // 8, 8, 128), axis=0),) + mass[g + 1:]
                return mass

            mass = expo(slice(W, W + T), T, (jnp.zeros((8, 128), F32),) * 2)
            mass = lax.fori_loop(0, NKB, lambda i, m: expo(pl.ds(pl.multiple_of(i * KB, KB), KB), KB, m), mass)
            inv = jnp.concatenate([1.0 / jnp.sum(m, axis=0, keepdims=True) for m in mass], axis=1)

            def weigh(i, out):
                ks = pl.ds(pl.multiple_of(i * KB, KB), KB)
                probs = (s_buf[ks, :] * inv).astype(BF16)
                return out + jnp.dot(vt[:, ks], probs, preferred_element_type=F32)

            probs = (s_buf[W:W + T, :] * inv).astype(BF16)
            out = jnp.dot(vt[:, W:W + T], probs, preferred_element_type=F32)
            out = lax.fori_loop(0, NKB, weigh, out)
            for g in range(2):
                o_buf[hp, :, g * 128:g * 128 + 128] = out[:, g * 128:g * 128 + 128].T.astype(BF16)
            return carry0

        lax.fori_loop(0, 2, half, 0)
        loads["wo"].wait()
        for n in range(NP):
            cols = slice(n * CW, n * CW + CW)
            part = jnp.dot(o_buf[0], wo[0:256, cols], preferred_element_type=F32)
            part = part + jnp.dot(o_buf[1], wo[256:512, cols], preferred_element_type=F32)
            rs_put(0, n, part)
            if n > 0:
                rs_pair(0, n - 1)
        rs_pair(0, NP - 1)
        loads["g2"].wait()

    pl.run_scoped(
        attention_phase,
        pltpu.VMEM((4 * D, 128), BF16),
        pltpu.VMEM((D, 768), BF16),
        pltpu.VMEM((W, 128), BF16),
        pltpu.VMEM((W, 128), BF16),
        pltpu.VMEM((128, W + T), BF16),
        pltpu.VMEM((512, D), BF16),
        pltpu.VMEM((T, 128), F32),
        pltpu.VMEM((T, 128), F32),
        pltpu.VMEM((512, 128), BF16),
        pltpu.VMEM((T, 128), BF16),
        pltpu.VMEM((T, 128), BF16),
        pltpu.VMEM((W + T, 256), F32),
        pltpu.VMEM((2, T, 256), BF16),
    )

    def mlp_phase(wd, acc_g, acc_u, u_buf):
        down_loads = [local(wd_hbm.at[:, pl.ds(n * CW, CW)], wd.at[:, pl.ds(n * CW, CW)], dsem.at[n]) for n in range(NP)]
        for ld in down_loads:
            ld.start()
        for n in range(NP):
            cols = slice(n * CW, n * CW + CW)
            hb[:, cols] = (xv[:, cols].astype(F32) + rs_sum(0, n)).astype(BF16)
        store_normed(hb, g2, xg2)
        ag_start(1, xg2)
        ag_finish(0, xg1)
        rs_finish(0)
        ag_relay(1, xg2, 0)
        for p in range(NP):
            gate_loads[2 * p].wait()
            gate_loads[2 * p + 1].wait()
            ag_arrive(1, xg2, p)
            rows = slice(p * CW, p * CW + CW)
            m = xg2[:, rows]
            gate = jnp.dot(m, wg[rows, :], preferred_element_type=F32)
            up = jnp.dot(m, wu[rows, :], preferred_element_type=F32)
            if p == 0:
                acc_g[...] = gate
                acc_u[...] = up
            elif p + 1 < NP:
                acc_g[...] += gate
                acc_u[...] += up
            else:
                gate = acc_g[...] + gate
                u_buf[...] = (gate / (1.0 + jnp.exp(-gate)) * (acc_u[...] + up)).astype(BF16)
            if p + 1 < NP:
                ag_relay(1, xg2, p + 1)
        for n in range(NP):
            cols = slice(n * CW, n * CW + CW)
            down_loads[n].wait()
            rs_put(1, n, jnp.dot(u_buf[...], wd[:, cols], preferred_element_type=F32))
            if n > 0:
                rs_pair(1, n - 1)
        rs_pair(1, NP - 1)
        ag_finish(1, xg2)
        for n in range(NP):
            cols = slice(n * CW, n * CW + CW)
            xo_ref[:, cols] = (hb[:, cols].astype(F32) + rs_sum(1, n)).astype(BF16)
        rs_finish(1)

    pl.run_scoped(
        mlp_phase,
        pltpu.VMEM((FF, D), BF16),
        pltpu.VMEM((T, FF), F32),
        pltpu.VMEM((T, FF), F32),
        pltpu.VMEM((T, FF), BF16),
    )


def cache_kernel(start_ref, kch_ref, vch_ref, kc_ref, vc_ref, ko_ref, vo_ref):
    block = pl.program_id(0)
    start = start_ref[0]
    slot = block * KB + lax.broadcasted_iota(jnp.int32, (KB, 128), 0)
    off = jnp.bitwise_and(slot - start, W - 1)
    tok = token_of_row(lax.broadcasted_iota(jnp.int32, (1, 128), 1))
    pick = (off == tok).astype(F32).astype(BF16)
    fresh = off < T
    for chunk, old, new in ((kch_ref, kc_ref, ko_ref), (vch_ref, vc_ref, vo_ref)):
        placed = jnp.dot(pick, chunk[...], preferred_element_type=F32)
        new[...] = jnp.where(fresh, placed, old[...].astype(F32)).astype(BF16)


def solution(mesh):
    row_spec = P('dp', 'tp', None)
    cache_spec = P('dp', None, 'tp', None)
    head_cols = P(None, 'tp', None)
    in_specs = (row_spec, P('dp'), cache_spec, cache_spec, P(), head_cols, head_cols, head_cols, P('tp', None, None), P(), P(None, 'tp'), P(None, 'tp'), P('tp', None))
    out_specs = (row_spec, cache_spec, cache_spec)

    def local_layer(x_in, start_pos, k_cache, v_cache, attn_gain, w_query, w_key, w_value, w_out, mlp_gain, w_gate, w_up, w_down):
        inv_freq = jnp.power(ROPE_BASE, -jnp.arange(0, 128, 2).astype(F32) / 128)
        tokens = token_of_row(jnp.arange(T))
        angles = (start_pos[0] + tokens).astype(F32)[:, None] * jnp.repeat(inv_freq, 2)[None, :]
        cos_t = jnp.cos(angles)
        sin_t = jnp.sin(angles) * jnp.where(jnp.arange(128) % 2 == 0, -1.0, 1.0)[None, :]
        any_spec = pl.BlockSpec(memory_space=pl.ANY)
        vmem_spec = pl.BlockSpec(memory_space=pltpu.VMEM)
        dma = pltpu.SemaphoreType.DMA
        kc2 = k_cache.reshape(W, 128)
        vc2 = v_cache.reshape(W, 128)
        x_out, k_chunk, v_chunk = pl.pallas_call(
            layer_kernel,
            out_shape=(
                jax.ShapeDtypeStruct((16, D), BF16),
                jax.ShapeDtypeStruct((T, 128), BF16),
                jax.ShapeDtypeStruct((T, 128), BF16),
            ),
            in_specs=[pl.BlockSpec(memory_space=pltpu.SMEM)] + [any_spec] * 14,
            out_specs=(vmem_spec, vmem_spec, vmem_spec),
            scratch_shapes=[
                pltpu.VMEM((16, D), BF16),
                pltpu.VMEM((32, 128), BF16),
                pltpu.VMEM((32, 128), BF16),
                pltpu.VMEM((D, FF), BF16),
                pltpu.VMEM((D, FF), BF16),
                pltpu.VMEM((T, D), BF16),
                pltpu.VMEM((T, D), BF16),
                pltpu.VMEM((2, NP, T, CW), BF16),
                pltpu.VMEM((2, NP, 64, CW), BF16),
                pltpu.VMEM((2, NP, 64, CW), BF16),
                pltpu.VMEM((2, 3, NP, 16, CW), BF16),
                pltpu.VMEM((16, D), BF16),
                dma((10,)),
                dma((2, NP)),
                dma((NP,)),
                dma((2, 4, NP)),
                dma((2, 4, NP)),
                dma((2, 4, NP)),
                dma((2, 4, NP)),
                dma((2, NP)),
                dma((2, NP)),
                dma((2, 4, NP)),
                dma((2, 4, NP)),
            ],
            compiler_params=pltpu.CompilerParams(collective_id=0, has_side_effects=True, vmem_limit_bytes=67043328),
            name="layer",
        )(
            start_pos, x_in.reshape(16, D), cos_t, sin_t, kc2, vc2, attn_gain.reshape(32, 128), w_query.reshape(4 * D, 128),
            w_key.reshape(D, 128), w_value.reshape(D, 128), w_out.reshape(512, D), mlp_gain.reshape(32, 128), w_gate, w_up, w_down,
        )
        chunk_spec = pl.BlockSpec((T, 128), lambda i: (0, 0))
        block_spec = pl.BlockSpec((KB, 128), lambda i: (i, 0))
        k_new, v_new = pl.pallas_call(
            cache_kernel,
            grid=(NKB,),
            out_shape=(jax.ShapeDtypeStruct((W, 128), BF16),) * 2,
            in_specs=[pl.BlockSpec(memory_space=pltpu.SMEM), chunk_spec, chunk_spec, block_spec, block_spec],
            out_specs=(block_spec, block_spec),
            name="caches",
        )(start_pos, k_chunk, v_chunk, kc2, vc2)
        return x_out.reshape(x_in.shape), k_new.reshape(k_cache.shape), v_new.reshape(v_cache.shape)

    return jax.shard_map(local_layer, mesh=mesh, in_specs=in_specs, out_specs=out_specs, check_vma=False)
```

time: 159 us -> 69.1 us (0.43)
  waiting for transfers between devices: 71.8 us -> 0 us
  Pallas kernels: 0 us -> 64.8 us
  matrix products: 41 us -> 0 us
  other arithmetic: 18.7 us -> 0.99 us
  between operations: 14.7 us -> 1.31 us
  local copies, waits for them, and re-layouts: 12.1 us -> 1.78 us
    pallas_call x0 -> x2, Pallas kernels: none -> 64.8 us  [the longest x1 58.3 us: local_layer(): pl.pallas_call(layer_kernel, out_shape=(jax.ShapeDtypeStruct((16, D), BF1...]
    reduce_scatter x2 -> x0, waiting for transfers between devices: 46.5 us -> none  [the longest x1 27.6 us: local_layer(): lax.psum_scatter(attn_part, 'tp', scatter_dimension=1, tiled=True)]
    dot_general x9 -> x0, matrix products: 41 us -> none  [the longest x1 15.1 us: local_layer(): jnp.einsum('btf,fd->btd', activated, w_down, preferred_element_type=jnp.f...]
    all_gather x2 -> x0, waiting for transfers between devices: 25.3 us -> none  [the longest x1 17.7 us: local_layer(): lax.all_gather(rms_norm(hidden, mlp_gain), 'tp', axis=1, tiled=True)]
    dot_general x2 -> x0, local copies, waits for them, and re-layouts: 10.1 us -> none  [the longest x1 9.56 us: project_qkv(): jnp.einsum('btd,dkge->btkge', normed, w_query4, preferred_element_type=jn...]
    select_n x2 -> x1, other arithmetic: 8.53 us -> 0.01 us  [local_layer(): jnp.where(jnp.arange(128) % 2 == 0, -1.0, 1.0)[None, :]]
    convert_element_type x6 -> x1, other arithmetic: 5.72 us -> 0.01 us  [local_layer(): (start_pos[0] + tokens).astype(F32)[:, None]]
    reduce_sum x4 -> x0, other arithmetic: 3.44 us -> none  [the longest x2 2.11 us: rms_norm(): jnp.mean(rows32 * rows32, axis=-1, keepdims=True) + NORM_EPS]
  transfers between devices with their start and end apart: 4 -> 0, of which waited for: 4 -> 0; matrix products, arithmetic and copies ran while one was open for 13% -> 0% of each run, Pallas kernels for 0% -> 0%
where the time goes in v1:
time: 69.1 us; the launch traced here: 68.9 us
  Pallas kernels  64.8 us (94%)
  local copies, waits for them, and re-layouts  1.78 us (3%)
  between operations  1.31 us (2%)
  other arithmetic  0.99 us (1%)
    pallas_call x1, Pallas kernels, local_layer(): pl.pallas_call(layer_kernel, out_shape=(jax.ShapeDtypeStruct((16, D), BF1...  58.3 us
    pallas_call x1, Pallas kernels, local_layer(): pl.pallas_call(cache_kernel, grid=(NKB,), out_shape=(jax.ShapeDtypeStruct...  6.48 us
    unnamed x1, local copies, waits for them, and re-layouts  1.57 us

profile of v1, /device:TPU:0, one launch (start us, length us, event | category | flops | bytes accessed | tf_op | source)
XLA Modules:
  0.0 68.9 jit_solution(13651271630860265945)
XLA Ops:
  1.3 0.1 broadcast_in_dim.13
  1.4 0.1 mul.53
  1.5 1.0 %fusion = (f32[128,128]{1,0:T(8,128)}, f32[128,128]{1,0:T(8,128)}) fusion(f32[128]{0:T(128)S(1)} %compare_select_fusion.2, f32[128]{0:T(128)S(1)} %mul.53, f32[128]{0:T(128)S(1)} %fusion.3), kind=kLoop, calls=%fused_computation.2 | loop fusion | flops 32768 | bytes 132608 | tf_op jit(solution)/shard_map/mul | solution.py:397
  2.5 58.3 %layer.1 = (bf16[16,4096]{1,0:T(8,128)(2,1)}, bf16[128,128]{1,0:T(8,128)(2,1)}, bf16[128,128]{1,0:T(8,128)(2,1)}) custom-call(s32[1]{0:T(128)} %copy.17.start_ref, bf16[16,4096]{1,0:T(8,128)(2,1)} %bitcast.22, f32[128,128]{1,0:T(8,128)} %get-tuple-element.14.cos_hbm, f32[128,128]{1,0:T(8,128)} %get-tuple-element.13.sin_hbm, bf16[4096,128]{1,0:T(8,128)(2,1)} %bitcast.14, ...), custom_call_target="tpu_custom_call" | custom-call | tf_op jit(solution)/shard_map/layer/pallas_call | solution.py:403
  60.8 6.5 %caches.1 = (bf16[4096,128]{1,0:T(8,128)(2,1)}, bf16[4096,128]{1,0:T(8,128)(2,1)}) custom-call(s32[1]{0:T(128)} %copy.17.start_ref, bf16[128,128]{1,0:T(8,128)(2,1)} %get-tuple-element.9.kch_ref, bf16[128,128]{1,0:T(8,128)(2,1)} %get-tuple-element.10.vch_ref, bf16[4096,128]{1,0:T(8,128)(2,1)} %bitcast.15, bf16[4096,128]{1,0:T(8,128)(2,1)} %bitcast.17), custom_call_target="tpu_custom_call" | custom-call | tf_op jit(solution)/shard_map/caches/pallas_call | solution.py:445
  67.3 1.6 %copy.18 = bf16[1,16,4096]{2,1,0:T(8,128)(2,1)} copy(bf16[1,16,4096]{2,1,0:T(8,128)(2,1)} %bitcast.23) | data formatting | bytes 262144
  (3 shorter events, 0.0 us)

commit v2 on v1

v2 whole, which is shorter than its diff:
```python
import functools

import jax
import numpy as np
import jax.numpy as jnp
from jax import lax
from jax.experimental import pallas as pl
from jax.experimental.pallas import tpu as pltpu
from jax.sharding import PartitionSpec as P

ROPE_BASE = 10000.0
NORM_EPS = 1e-5
BF16 = jnp.bfloat16
F32 = jnp.float32
D = 4096
T = 128
FF = 1792
W = 4096
NP = 8
VMEM_LIMIT = 64000000
CW = D // NP
KB = 512
NKB = W // KB


def token_of_row(row):
    core = row // 64
    chip = (row // 16) % 4
    return 32 * chip + 16 * core + row % 16


def layer_kernel(start_ref, x_hbm, freq_hbm, kc_hbm, vc_hbm, g1_hbm, wq_hbm, wk_hbm, wv_hbm, wo_hbm, g2_hbm, wg_hbm, wu_hbm, wd_hbm,
                 xo_ref, kn_ref, vn_ref,
                 xv, g1, g2, wg, wu, xg1, xg2, pbuf, ra, sb, rb, hb,
                 lsem, wsem, dsem, send_sem, recv_sem, fsend_sem, frecv_sem, asend_sem, arecv_sem, bsend_sem, brecv_sem):
    me = lax.axis_index("tp")
    core = me % 2
    chip = me // 2
    other = 1 - core
    partner = 2 * chip + other
    flip1 = chip + 1 - 2 * (chip % 2)
    flip2 = chip + 2 - 4 * (chip // 2)
    flip3 = 3 - chip
    chips = (chip, flip1, flip2, flip3)
    my_rows = pl.ds(pl.multiple_of(64 * core + 16 * chip, 16), 16)

    def rows_of(c, q):
        return pl.ds(pl.multiple_of(64 * c + 16 * q, 16), 16)

    def remote(src, dst, ssem, rsem, dev):
        return pltpu.make_async_remote_copy(src_ref=src, dst_ref=dst, send_sem=ssem, recv_sem=rsem, device_id={"tp": dev}, device_id_type=pl.DeviceIdType.MESH)

    def local(src, dst, sem):
        return pltpu.make_async_copy(src, dst, sem)

    def ag_direct(ph, xg, r, p):
        cols = pl.ds(p * CW, CW)
        return remote(xg.at[my_rows, cols], xg.at[my_rows, cols], send_sem.at[ph, r, p], recv_sem.at[ph, r, p], 2 * chips[r] + core)

    def ag_direct_in(ph, xg, r, p):
        ref = xg.at[rows_of(core, chips[r]), pl.ds(p * CW, CW)]
        return remote(ref, ref, send_sem.at[ph, r, p], recv_sem.at[ph, r, p], 2 * chips[r] + core)

    def ag_forward(ph, xg, r, p):
        ref = xg.at[rows_of(core, chips[r]), pl.ds(p * CW, CW)]
        return remote(ref, ref, fsend_sem.at[ph, r, p], frecv_sem.at[ph, r, p], partner)

    def ag_forward_in(ph, xg, r, p):
        ref = xg.at[rows_of(other, chips[r]), pl.ds(p * CW, CW)]
        return remote(ref, ref, fsend_sem.at[ph, r, p], frecv_sem.at[ph, r, p], partner)

    def ag_start(ph, xg):
        for p in range(NP):
            for r in (3, 1, 2):
                ag_direct(ph, xg, r, p).start()
            ag_forward(ph, xg, 0, p).start()

    def ag_relay(ph, xg, p):
        for r in (1, 2, 3):
            ag_direct_in(ph, xg, r, p).wait_recv()
            ag_forward(ph, xg, r, p).start()

    def ag_arrive(ph, xg, p):
        for r in (0, 1, 2, 3):
            ag_forward_in(ph, xg, r, p).wait_recv()

    def ag_finish(ph, xg):
        for p in range(NP):
            for r in (1, 2, 3):
                ag_direct(ph, xg, r, p).wait_send()
            for r in (0, 1, 2, 3):
                ag_forward(ph, xg, r, p).wait_send()

    def rs_a(ph, n):
        return remote(pbuf.at[ph, n, pl.ds(pl.multiple_of(64 * other, 64), 64), :], ra.at[ph, n], asend_sem.at[ph, n], arecv_sem.at[ph, n], partner)

    def rs_b(ph, n, r):
        return remote(sb.at[ph, n, pl.ds(pl.multiple_of(16 * chips[r], 16), 16), :], rb.at[ph, r - 1, n], bsend_sem.at[ph, r, n], brecv_sem.at[ph, r, n], 2 * chips[r] + core)

    def rs_put(ph, n, part):
        pbuf[ph, n] = part.astype(BF16)
        rs_a(ph, n).start()

    def rs_pair(ph, n):
        rs_a(ph, n).wait_recv()
        own = pbuf[ph, n, pl.ds(pl.multiple_of(64 * core, 64), 64), :].astype(F32)
        sb[ph, n] = (own + ra[ph, n].astype(F32)).astype(BF16)
        for r in (3, 1, 2):
            rs_b(ph, n, r).start()

    def rs_sum(ph, n):
        total = sb[ph, n, pl.ds(pl.multiple_of(16 * chip, 16), 16), :].astype(F32)
        for r in (1, 2, 3):
            rs_b(ph, n, r).wait_recv()
            total = total + rb[ph, r - 1, n].astype(F32)
        return total

    def rs_finish(ph):
        for n in range(NP):
            rs_a(ph, n).wait_send()
            for r in (1, 2, 3):
                rs_b(ph, n, r).wait_send()

    def normed(rows, gain):
        ms = jnp.zeros((16, 128), F32)
        for j in range(32):
            v = rows[:, 128 * j:128 * j + 128].astype(F32)
            ms = ms + v * v
        inv = lax.rsqrt(jnp.sum(ms, axis=-1, keepdims=True) * (1.0 / D) + NORM_EPS)
        return inv

    def store_normed(src, gain, dst):
        inv = normed(src, gain)
        for j in range(32):
            cols = slice(128 * j, 128 * j + 128)
            val = src[:, cols].astype(F32) * inv * gain[j:j + 1, :].astype(F32)
            dst[my_rows, cols] = val.astype(BF16)

    gate_loads = []
    for p in range(NP):
        gate_loads.append(local(wg_hbm.at[pl.ds(p * CW, CW), :], wg.at[pl.ds(p * CW, CW), :], wsem.at[0, p]))
        gate_loads.append(local(wu_hbm.at[pl.ds(p * CW, CW), :], wu.at[pl.ds(p * CW, CW), :], wsem.at[1, p]))

    def attention_phase(kc, vc, vt, wo, freqv, qs, kch, vch, bias, o_buf):
        loads = {
            "x": local(x_hbm, xv, lsem.at[0]),
            "g1": local(g1_hbm, g1, lsem.at[1]),
            "freq": local(freq_hbm, freqv, lsem.at[6]),
            "vc": local(vc_hbm, vc, lsem.at[4]),
            "kc": local(kc_hbm, kc, lsem.at[5]),
            "wo": local(wo_hbm, wo, lsem.at[8]),
            "g2": local(g2_hbm, g2, lsem.at[9]),
        }
        loads["x"].start()
        loads["g1"].start()
        barrier = pltpu.get_barrier_semaphore()
        for dev in (partner, 2 * flip1 + core, 2 * flip2 + core, 2 * flip3 + core):
            pl.semaphore_signal(barrier, inc=1, device_id={"tp": dev}, device_id_type=pl.DeviceIdType.MESH)
        start = start_ref[0]
        tok_lane = token_of_row(lax.broadcasted_iota(jnp.int32, (1, 128), 1))

        def projection_phase(wq4, wqkv):
            wk_load = local(wk_hbm, wqkv.at[:, pl.ds(512, 128)], lsem.at[2])
            wv_load = local(wv_hbm, wqkv.at[:, pl.ds(640, 128)], lsem.at[3])
            wq_loads = [local(wq_hbm.at[pl.ds(p * 4 * CW, 4 * CW), :], wq4.at[pl.ds(p * 4 * CW, 4 * CW), :], dsem.at[p]) for p in range(NP)]
            for ld in wq_loads:
                ld.start()
            loads["vc"].start()
            loads["freq"].start()
            wk_load.start()
            wv_load.start()
            for name in ("kc", "wo", "g2"):
                loads[name].start()

            loads["x"].wait()
            loads["g1"].wait()
            store_normed(xv, g1, xg1)
            pl.semaphore_wait(barrier, 4)
            ag_start(0, xg1)

            ri = lax.broadcasted_iota(jnp.int32, (256, 256), 0)
            ci = lax.broadcasted_iota(jnp.int32, (256, 256), 1)
            perm = (ci == 4 * (ri % 64) + ri // 64).astype(F32).astype(BF16)

            def split_heads(p):
                wq_loads[p].wait()

                def body(i, carry):
                    base = p * (CW // 64) + 2 * i
                    rows4 = jnp.concatenate([wq4[pl.ds(pl.multiple_of((base + k) * 256, 256), 256), :] for k in range(2)], axis=1)
                    out = jnp.dot(perm, rows4, preferred_element_type=F32).astype(BF16)
                    for k in range(2):
                        for h in range(4):
                            wqkv[pl.ds(pl.multiple_of((base + k) * 64, 64), 64), h * 128:h * 128 + 128] = out[64 * h:64 * h + 64, k * 128:k * 128 + 128]
                    return carry

                for i in range(CW // 128):
                    body(i, 0)

            split_heads(0)
            ag_relay(0, xg1, 0)
            loads["vc"].wait()

            def flip_values(i, carry):
                ks = pl.ds(pl.multiple_of(i * KB, KB), KB)
                vt[:, ks] = vc[ks, :].astype(F32).T.astype(BF16)
                slot = i * KB + lax.broadcasted_iota(jnp.int32, (KB, 128), 0)
                off = jnp.bitwise_and(slot - start, W - 1)
                keep = jnp.where(off >= W - start, off, -1) > tok_lane
                bias[ks, :] = jnp.where(keep, 0.0, -jnp.inf)
                return carry

            loads["freq"].wait()
            tok_row = token_of_row(lax.broadcasted_iota(jnp.int32, (T, 128), 0))
            angles = (start + tok_row).astype(F32) * freqv[0:1, :]
            cos_t = jnp.cos(angles)
            lane = lax.broadcasted_iota(jnp.int32, (T, 128), 1)
            even = lane % 2 == 0
            sin_t = jnp.sin(angles)
            sin_t = jnp.where(even, -sin_t, sin_t)
            wk_load.wait()
            wv_load.wait()
            acc = jnp.zeros((T, 768), F32)
            for p in range(NP):
                if p + 1 < NP:
                    split_heads(p + 1)
                flip_values(p, 0)
                ag_arrive(0, xg1, p)
                cols = slice(p * CW, p * CW + CW)
                acc = acc + jnp.dot(xg1[:, cols], wqkv[cols, :], preferred_element_type=F32)
                if p + 1 < NP:
                    ag_relay(0, xg1, p + 1)
            for ld in gate_loads:
                ld.start()

            def rotate(v):
                swapped = jnp.where(even, pltpu.roll(v, 127, 1), pltpu.roll(v, 1, 1))
                return v * cos_t + swapped * sin_t

            for h in range(4):
                qs[h * 128:h * 128 + 128, :] = rotate(acc[:, h * 128:h * 128 + 128]).astype(BF16)
            kch[...] = rotate(acc[:, 512:640]).astype(BF16)
            v_new = acc[:, 640:768].astype(BF16)
            vch[...] = v_new
            vt[:, W:W + T] = v_new.astype(F32).T.astype(BF16)

        pl.run_scoped(
            projection_phase,
            pltpu.VMEM((4 * D, 128), BF16),
            pltpu.VMEM((D, 768), BF16),
        )
        loads["kc"].wait()
        factor = (128.0 ** -0.5) * 1.4426950408889634

        def softmax_phase(s_buf):
            queries = qs[...]
            tops, masses = [], []
            for b in range(NKB + 1):
                n = KB if b < NKB else T
                ks = slice(b * KB, b * KB + n)
                keys = kc[ks, :] if b < NKB else kch[...]
                st = lax.dot_general(keys, queries, (((1,), (1,)), ((), ())), preferred_element_type=F32)
                if b < NKB:
                    shift = bias[ks, :]
                else:
                    shift = jnp.where(token_of_row(lax.broadcasted_iota(jnp.int32, (T, 128), 0)) <= tok_lane, 0.0, -jnp.inf)
                top, mass = [], []
                for g in range(4):
                    gs = slice(g * 128, g * 128 + 128)
                    part = st[:, gs] + shift
                    s_buf[ks, gs] = part
                    t = jnp.max(jnp.max(part.reshape(n // 8, 8, 128), axis=0), axis=0, keepdims=True)
                    t = jnp.maximum(t, jnp.finfo(F32).min)
                    e = jnp.exp2((s_buf[ks, gs] - t) * factor)
                    s_buf[ks, gs] = e
                    mass.append(jnp.sum(jnp.sum(e.reshape(n // 8, 8, 128), axis=0), axis=0, keepdims=True))
                    top.append(t)
                tops.append(jnp.concatenate(top, axis=1))
                masses.append(jnp.concatenate(mass, axis=1))
            best = functools.reduce(jnp.maximum, tops)
            scales = [jnp.exp2((t - best) * factor) for t in tops]
            total = sum(m * sc for m, sc in zip(masses, scales))
            inv = 1.0 / total
            out = None
            for b in range(NKB + 1):
                n = KB if b < NKB else T
                ks = slice(b * KB, b * KB + n)
                probs = (s_buf[ks, :] * (scales[b] * inv)).astype(BF16)
                part = jnp.dot(vt[:, ks], probs, preferred_element_type=F32)
                out = part if out is None else out + part
            for g in range(4):
                o_buf[:, g * 128:g * 128 + 128] = out[:, g * 128:g * 128 + 128].T.astype(BF16)

        pl.run_scoped(softmax_phase, pltpu.VMEM((W + T, 512), F32))
        loads["wo"].wait()
        for n in range(NP):
            cols = slice(n * CW, n * CW + CW)
            rs_put(0, n, jnp.dot(o_buf[...], wo[:, cols], preferred_element_type=F32))
            if n > 0:
                rs_pair(0, n - 1)
        rs_pair(0, NP - 1)
        loads["g2"].wait()

        chunk = jnp.concatenate([kch[...], vch[...]], axis=1)

        def merge(i, carry):
            ks = pl.ds(pl.multiple_of(i * KB, KB), KB)
            slot = i * KB + lax.broadcasted_iota(jnp.int32, (KB, 128), 0)
            off = jnp.bitwise_and(slot - start, W - 1)
            pick = (off == tok_lane).astype(F32).astype(BF16)
            placed = jnp.dot(pick, chunk, preferred_element_type=F32)
            fresh = off < T
            kn_ref[ks, :] = jnp.where(fresh, placed[:, 0:128], kc[ks, :].astype(F32)).astype(BF16)
            vn_ref[ks, :] = jnp.where(fresh, placed[:, 128:256], vc[ks, :].astype(F32)).astype(BF16)
            return carry

        lax.fori_loop(0, NKB, merge, 0)

    pl.run_scoped(
        attention_phase,
        pltpu.VMEM((W, 128), BF16),
        pltpu.VMEM((W, 128), BF16),
        pltpu.VMEM((128, W + T), BF16),
        pltpu.VMEM((512, D), BF16),
        pltpu.VMEM((8, 128), F32),
        pltpu.VMEM((512, 128), BF16),
        pltpu.VMEM((T, 128), BF16),
        pltpu.VMEM((T, 128), BF16),
        pltpu.VMEM((W, 128), F32),
        pltpu.VMEM((T, 512), BF16),
    )

    def mlp_phase(wd, acc_g, acc_u, u_buf):
        down_loads = [local(wd_hbm.at[:, pl.ds(n * CW, CW)], wd.at[:, pl.ds(n * CW, CW)], dsem.at[n]) for n in range(NP)]
        for ld in down_loads:
            ld.start()
        for n in range(NP):
            cols = slice(n * CW, n * CW + CW)
            hb[:, cols] = (xv[:, cols].astype(F32) + rs_sum(0, n)).astype(BF16)
        store_normed(hb, g2, xg2)
        ag_start(1, xg2)
        ag_finish(0, xg1)
        rs_finish(0)
        ag_relay(1, xg2, 0)
        for p in range(NP):
            gate_loads[2 * p].wait()
            gate_loads[2 * p + 1].wait()
            ag_arrive(1, xg2, p)
            rows = slice(p * CW, p * CW + CW)
            m = xg2[:, rows]
            gate = jnp.dot(m, wg[rows, :], preferred_element_type=F32)
            up = jnp.dot(m, wu[rows, :], preferred_element_type=F32)
            if p == 0:
                acc_g[...] = gate
                acc_u[...] = up
            elif p + 1 < NP:
                acc_g[...] += gate
                acc_u[...] += up
            else:
                gate = acc_g[...] + gate
                u_buf[...] = (gate / (1.0 + jnp.exp(-gate)) * (acc_u[...] + up)).astype(BF16)
            if p + 1 < NP:
                ag_relay(1, xg2, p + 1)
        for n in range(NP):
            cols = slice(n * CW, n * CW + CW)
            down_loads[n].wait()
            rs_put(1, n, jnp.dot(u_buf[...], wd[:, cols], preferred_element_type=F32))
            if n > 0:
                rs_pair(1, n - 1)
        rs_pair(1, NP - 1)
        ag_finish(1, xg2)
        for n in range(NP):
            cols = slice(n * CW, n * CW + CW)
            xo_ref[:, cols] = (hb[:, cols].astype(F32) + rs_sum(1, n)).astype(BF16)
        rs_finish(1)

    pl.run_scoped(
        mlp_phase,
        pltpu.VMEM((FF, D), BF16),
        pltpu.VMEM((T, FF), F32),
        pltpu.VMEM((T, FF), F32),
        pltpu.VMEM((T, FF), BF16),
    )


def solution(mesh):
    row_spec = P('dp', 'tp', None)
    cache_spec = P('dp', None, 'tp', None)
    head_cols = P(None, 'tp', None)
    in_specs = (row_spec, P('dp'), cache_spec, cache_spec, P(), head_cols, head_cols, head_cols, P('tp', None, None), P(), P(None, 'tp'), P(None, 'tp'), P('tp', None))
    out_specs = (row_spec, cache_spec, cache_spec)

    def local_layer(x_in, start_pos, k_cache, v_cache, attn_gain, w_query, w_key, w_value, w_out, mlp_gain, w_gate, w_up, w_down):
        freq = np.repeat(ROPE_BASE ** (-np.arange(0, 128, 2) / 128.0), 2).astype(np.float32)
        freq = jnp.asarray(np.tile(freq[None, :], (8, 1)))
        any_spec = pl.BlockSpec(memory_space=pl.ANY)
        vmem_spec = pl.BlockSpec(memory_space=pltpu.VMEM)
        dma = pltpu.SemaphoreType.DMA
        kc2 = k_cache.reshape(W, 128)
        vc2 = v_cache.reshape(W, 128)
        x_out, k_new, v_new = pl.pallas_call(
            layer_kernel,
            out_shape=(pltpu.VMEM((16, D), BF16), pltpu.VMEM((W, 128), BF16), pltpu.VMEM((W, 128), BF16)),
            in_specs=[pl.BlockSpec(memory_space=pltpu.SMEM)] + [any_spec] * 13,
            out_specs=(vmem_spec, vmem_spec, vmem_spec),
            scratch_shapes=[
                pltpu.VMEM((16, D), BF16),
                pltpu.VMEM((32, 128), BF16),
                pltpu.VMEM((32, 128), BF16),
                pltpu.VMEM((D, FF), BF16),
                pltpu.VMEM((D, FF), BF16),
                pltpu.VMEM((T, D), BF16),
                pltpu.VMEM((T, D), BF16),
                pltpu.VMEM((2, NP, T, CW), BF16),
                pltpu.VMEM((2, NP, 64, CW), BF16),
                pltpu.VMEM((2, NP, 64, CW), BF16),
                pltpu.VMEM((2, 3, NP, 16, CW), BF16),
                pltpu.VMEM((16, D), BF16),
                dma((10,)),
                dma((2, NP)),
                dma((NP,)),
                dma((2, 4, NP)),
                dma((2, 4, NP)),
                dma((2, 4, NP)),
                dma((2, 4, NP)),
                dma((2, NP)),
                dma((2, NP)),
                dma((2, 4, NP)),
                dma((2, 4, NP)),
            ],
            compiler_params=pltpu.CompilerParams(collective_id=0, has_side_effects=True, vmem_limit_bytes=VMEM_LIMIT),
            name="layer",
        )(
            start_pos, x_in.reshape(16, D), freq, kc2, vc2, attn_gain.reshape(32, 128), w_query.reshape(4 * D, 128),
            w_key.reshape(D, 128), w_value.reshape(D, 128), w_out.reshape(512, D), mlp_gain.reshape(32, 128), w_gate, w_up, w_down,
        )
        return x_out.reshape(x_in.shape), k_new.reshape(k_cache.shape), v_new.reshape(v_cache.shape)

    return jax.shard_map(local_layer, mesh=mesh, in_specs=in_specs, out_specs=out_specs, check_vma=False)
```

time: 69.1 us -> 63 us (0.912)
  Pallas kernels: 64.8 us -> 59 us
  other arithmetic: 0.99 us -> 0 us
  local copies, waits for them, and re-layouts: 1.78 us -> 2.6 us
    pallas_call x2 -> x1, Pallas kernels: 64.8 us -> 59 us  [local_layer(): pl.pallas_call(layer_kernel, out_shape=(pltpu.VMEM((16, D), BF16), pltpu....]
    unnamed x1 -> x3, local copies, waits for them, and re-layouts: 1.57 us -> 2.6 us
    mul x1 -> x0, other arithmetic: 0.97 us -> none  [local_layer(): jnp.sin(angles) * jnp.where(jnp.arange(128) % 2 == 0, -1.0, 1.0)[None, :]]
where the time goes in v2:
time: 63 us; the launch traced here: 62.9 us
  Pallas kernels  59 us (94%)
  local copies, waits for them, and re-layouts  2.6 us (4%)
  between operations  1.29 us (2%)
    pallas_call x1, Pallas kernels, local_layer(): pl.pallas_call(layer_kernel, out_shape=(pltpu.VMEM((16, D), BF16), pltpu....  59 us
    unnamed x3, local copies, waits for them, and re-layouts  2.6 us

profile of v2, /device:TPU:0, one launch (start us, length us, event | category | flops | bytes accessed | tf_op | source)
XLA Modules:
  0.0 62.9 jit_solution(14568717119083091522)
XLA Ops:
  1.3 59.0 %layer.1 = (bf16[16,4096]{1,0:T(8,128)(2,1)S(1)}, bf16[4096,128]{1,0:T(8,128)(2,1)S(1)}, bf16[4096,128]{1,0:T(8,128)(2,1)S(1)}) custom-call(s32[1]{0:T(128)S(6)} %copy.23.start_ref, bf16[16,4096]{1,0:T(8,128)(2,1)} %bitcast.21, f32[8,128]{1,0:T(8,128)} %constant.2.clone.freq_hbm, bf16[4096,128]{1,0:T(8,128)(2,1)} %bitcast.17, bf16[4096,128]{1,0:T(8,128)(2,1)} %bitcast.18, ...), custom_call_target="tpu_custom_call" | custom-call | tf_op jit(solution)/shard_map/layer/pallas_call | solution.py:401
  60.3 0.7 %copy.20 = bf16[1,16,4096]{2,1,0:T(8,128)(2,1)} copy(bf16[1,16,4096]{2,1,0:T(8,128)(2,1)S(1)} %bitcast.14) | data formatting | bytes 262144
  61.0 1.0 %copy.21 = bf16[1,4096,1,128]{3,1,2,0:T(8,128)(2,1)} copy(bf16[1,4096,1,128]{3,1,2,0:T(8,128)(2,1)S(1)} %bitcast.13) | data formatting | bytes 2097152
  61.9 1.0 %copy.22 = bf16[1,4096,1,128]{3,1,2,0:T(8,128)(2,1)} copy(bf16[1,4096,1,128]{3,1,2,0:T(8,128)(2,1)S(1)} %bitcast.12) | data formatting | bytes 2097152

commit v3 on v2

--- a/solution.py
+++ b/solution.py
@@ -29,9 +29,9 @@
     return 32 * chip + 16 * core + row % 16
 
 
-def layer_kernel(start_ref, x_hbm, freq_hbm, kc_hbm, vc_hbm, g1_hbm, wq_hbm, wk_hbm, wv_hbm, wo_hbm, g2_hbm, wg_hbm, wu_hbm, wd_hbm,
+def layer_kernel(start_hbm, x_hbm, freq_hbm, kc_hbm, vc_hbm, g1_hbm, wq_hbm, wk_hbm, wv_hbm, wo_hbm, g2_hbm, wg_hbm, wu_hbm, wd_hbm,
                  xo_ref, kn_ref, vn_ref,
-                 xv, g1, g2, wg, wu, xg1, xg2, pbuf, ra, sb, rb, hb,
+                 start_ref, xv, g1, g2, wg, wu, xg1, xg2, pbuf, ra, sb, rb, hb,
                  lsem, wsem, dsem, send_sem, recv_sem, fsend_sem, frecv_sem, asend_sem, arecv_sem, bsend_sem, brecv_sem):
     me = lax.axis_index("tp")
     core = me % 2
@@ -150,13 +150,13 @@
             "kc": local(kc_hbm, kc, lsem.at[5]),
             "wo": local(wo_hbm, wo, lsem.at[8]),
             "g2": local(g2_hbm, g2, lsem.at[9]),
+            "start": local(start_hbm, start_ref, lsem.at[7]),
         }
         loads["x"].start()
         loads["g1"].start()
         barrier = pltpu.get_barrier_semaphore()
         for dev in (partner, 2 * flip1 + core, 2 * flip2 + core, 2 * flip3 + core):
             pl.semaphore_signal(barrier, inc=1, device_id={"tp": dev}, device_id_type=pl.DeviceIdType.MESH)
-        start = start_ref[0]
         tok_lane = token_of_row(lax.broadcasted_iota(jnp.int32, (1, 128), 1))
 
         def projection_phase(wq4, wqkv):
@@ -167,6 +167,7 @@
                 ld.start()
             loads["vc"].start()
             loads["freq"].start()
+            loads["start"].start()
             wk_load.start()
             wv_load.start()
             for name in ("kc", "wo", "g2"):
@@ -197,8 +198,6 @@
                 for i in range(CW // 128):
                     body(i, 0)
 
-            split_heads(0)
-            ag_relay(0, xg1, 0)
             loads["vc"].wait()
 
             def flip_values(i, carry):
@@ -210,6 +209,12 @@
                 bias[ks, :] = jnp.where(keep, 0.0, -jnp.inf)
                 return carry
 
+            loads["start"].wait()
+            start = start_ref[0]
+            for p in range(4):
+                split_heads(p)
+            for p in range(6):
+                flip_values(p, 0)
             loads["freq"].wait()
             tok_row = token_of_row(lax.broadcasted_iota(jnp.int32, (T, 128), 0))
             angles = (start + tok_row).astype(F32) * freqv[0:1, :]
@@ -221,15 +226,18 @@
             wk_load.wait()
             wv_load.wait()
             acc = jnp.zeros((T, 768), F32)
+            ag_relay(0, xg1, 0)
+            ag_relay(0, xg1, 1)
             for p in range(NP):
-                if p + 1 < NP:
-                    split_heads(p + 1)
-                flip_values(p, 0)
+                if p + 2 < NP:
+                    ag_relay(0, xg1, p + 2)
+                if p + 4 < NP:
+                    split_heads(p + 4)
+                if p < 2:
+                    flip_values(p + 6, 0)
                 ag_arrive(0, xg1, p)
                 cols = slice(p * CW, p * CW + CW)
                 acc = acc + jnp.dot(xg1[:, cols], wqkv[cols, :], preferred_element_type=F32)
-                if p + 1 < NP:
-                    ag_relay(0, xg1, p + 1)
             for ld in gate_loads:
                 ld.start()
 
@@ -314,6 +322,7 @@
             vn_ref[ks, :] = jnp.where(fresh, placed[:, 128:256], vc[ks, :].astype(F32)).astype(BF16)
             return carry
 
+        start = start_ref[0]
         lax.fori_loop(0, NKB, merge, 0)
 
     pl.run_scoped(
@@ -342,7 +351,10 @@
         ag_finish(0, xg1)
         rs_finish(0)
         ag_relay(1, xg2, 0)
+        ag_relay(1, xg2, 1)
         for p in range(NP):
+            if p + 2 < NP:
+                ag_relay(1, xg2, p + 2)
             gate_loads[2 * p].wait()
             gate_loads[2 * p + 1].wait()
             ag_arrive(1, xg2, p)
@@ -359,8 +371,6 @@
             else:
                 gate = acc_g[...] + gate
                 u_buf[...] = (gate / (1.0 + jnp.exp(-gate)) * (acc_u[...] + up)).astype(BF16)
-            if p + 1 < NP:
-                ag_relay(1, xg2, p + 1)
         for n in range(NP):
             cols = slice(n * CW, n * CW + CW)
             down_loads[n].wait()
@@ -401,9 +411,10 @@
         x_out, k_new, v_new = pl.pallas_call(
             layer_kernel,
             out_shape=(pltpu.VMEM((16, D), BF16), pltpu.VMEM((W, 128), BF16), pltpu.VMEM((W, 128), BF16)),
-            in_specs=[pl.BlockSpec(memory_space=pltpu.SMEM)] + [any_spec] * 13,
+            in_specs=[any_spec] * 14,
             out_specs=(vmem_spec, vmem_spec, vmem_spec),
             scratch_shapes=[
+                pltpu.SMEM((1,), jnp.int32),
                 pltpu.VMEM((16, D), BF16),
                 pltpu.VMEM((32, 128), BF16),
                 pltpu.VMEM((32, 128), BF16),

time: 63 us -> 53 us (0.84)
  Pallas kernels: 59 us -> 49 us
    pallas_call x1, Pallas kernels: 59 us -> 49 us  [local_layer(): pl.pallas_call(layer_kernel, out_shape=(pltpu.VMEM((16, D), BF16), pltpu....]
where the time goes in v3:
time: 53 us; the launch traced here: 52.9 us
  Pallas kernels  49 us (92%)
  local copies, waits for them, and re-layouts  2.6 us (5%)
  between operations  1.29 us (2%)
    pallas_call x1, Pallas kernels, local_layer(): pl.pallas_call(layer_kernel, out_shape=(pltpu.VMEM((16, D), BF16), pltpu....  49 us
    unnamed x3, local copies, waits for them, and re-layouts  2.6 us

profile of v3, /device:TPU:0, one launch (start us, length us, event | category | flops | bytes accessed | tf_op | source)
XLA Modules:
  0.0 52.9 jit_solution(3536852780812881640)
XLA Ops:
  1.3 49.0 %layer.1 = (bf16[16,4096]{1,0:T(8,128)(2,1)S(1)}, bf16[4096,128]{1,0:T(8,128)(2,1)S(1)}, bf16[4096,128]{1,0:T(8,128)(2,1)S(1)}) custom-call(s32[1]{0:T(128)S(6)} %copy.23.start_hbm, bf16[16,4096]{1,0:T(8,128)(2,1)} %bitcast.21, f32[8,128]{1,0:T(8,128)} %constant.2.clone.freq_hbm, bf16[4096,128]{1,0:T(8,128)(2,1)} %bitcast.17, bf16[4096,128]{1,0:T(8,128)(2,1)} %bitcast.18, ...), custom_call_target="tpu_custom_call" | custom-call | tf_op jit(solution)/shard_map/layer/pallas_call | solution.py:411
  50.3 0.7 %copy.20 = bf16[1,16,4096]{2,1,0:T(8,128)(2,1)} copy(bf16[1,16,4096]{2,1,0:T(8,128)(2,1)S(1)} %bitcast.14) | data formatting | bytes 262144
  50.9 1.0 %copy.21 = bf16[1,4096,1,128]{3,1,2,0:T(8,128)(2,1)} copy(bf16[1,4096,1,128]{3,1,2,0:T(8,128)(2,1)S(1)} %bitcast.13) | data formatting | bytes 2097152
  51.9 1.0 %copy.22 = bf16[1,4096,1,128]{3,1,2,0:T(8,128)(2,1)} copy(bf16[1,4096,1,128]{3,1,2,0:T(8,128)(2,1)S(1)} %bitcast.12) | data formatting | bytes 2097152

commit v4 on v3

--- a/solution.py
+++ b/solution.py
@@ -19,12 +19,15 @@
 NP = 8
 VMEM_LIMIT = 64000000
 CW = D // NP
+NQ = 4
+CQ = D // NQ
+AHEAD = 1
 KB = 512
 NKB = W // KB
 
 
 def token_of_row(row):
-    core = row // 64
+    core = 1 - row // 64
     chip = (row // 16) % 4
     return 32 * chip + 16 * core + row % 16
 
@@ -42,10 +45,10 @@
     flip2 = chip + 2 - 4 * (chip // 2)
     flip3 = 3 - chip
     chips = (chip, flip1, flip2, flip3)
-    my_rows = pl.ds(pl.multiple_of(64 * core + 16 * chip, 16), 16)
+    my_rows = pl.ds(pl.multiple_of(64 * other + 16 * chip, 16), 16)
 
     def rows_of(c, q):
-        return pl.ds(pl.multiple_of(64 * c + 16 * q, 16), 16)
+        return pl.ds(pl.multiple_of(64 * (1 - c) + 16 * q, 16), 16)
 
     def remote(src, dst, ssem, rsem, dev):
         return pltpu.make_async_remote_copy(src_ref=src, dst_ref=dst, send_sem=ssem, recv_sem=rsem, device_id={"tp": dev}, device_id_type=pl.DeviceIdType.MESH)
@@ -53,24 +56,29 @@
     def local(src, dst, sem):
         return pltpu.make_async_copy(src, dst, sem)
 
+    widths = (CW, CQ)
+
+    def piece(ph, xg, c, r, p):
+        return xg.at[rows_of(c, chips[r]), pl.ds(p * widths[ph], widths[ph])]
+
     def ag_direct(ph, xg, r, p):
-        cols = pl.ds(p * CW, CW)
-        return remote(xg.at[my_rows, cols], xg.at[my_rows, cols], send_sem.at[ph, r, p], recv_sem.at[ph, r, p], 2 * chips[r] + core)
+        ref = piece(ph, xg, core, 0, p)
+        return remote(ref, ref, send_sem.at[ph, r, p], recv_sem.at[ph, r, p], 2 * chips[r] + core)
 
     def ag_direct_in(ph, xg, r, p):
-        ref = xg.at[rows_of(core, chips[r]), pl.ds(p * CW, CW)]
+        ref = piece(ph, xg, core, r, p)
         return remote(ref, ref, send_sem.at[ph, r, p], recv_sem.at[ph, r, p], 2 * chips[r] + core)
 
     def ag_forward(ph, xg, r, p):
-        ref = xg.at[rows_of(core, chips[r]), pl.ds(p * CW, CW)]
+        ref = piece(ph, xg, core, r, p)
         return remote(ref, ref, fsend_sem.at[ph, r, p], frecv_sem.at[ph, r, p], partner)
 
     def ag_forward_in(ph, xg, r, p):
-        ref = xg.at[rows_of(other, chips[r]), pl.ds(p * CW, CW)]
+        ref = piece(ph, xg, other, r, p)
         return remote(ref, ref, fsend_sem.at[ph, r, p], frecv_sem.at[ph, r, p], partner)
 
     def ag_start(ph, xg):
-        for p in range(NP):
+        for p in range(D // widths[ph]):
             for r in (3, 1, 2):
                 ag_direct(ph, xg, r, p).start()
             ag_forward(ph, xg, 0, p).start()
@@ -85,28 +93,39 @@
             ag_forward_in(ph, xg, r, p).wait_recv()
 
     def ag_finish(ph, xg):
-        for p in range(NP):
+        for p in range(D // widths[ph]):
             for r in (1, 2, 3):
                 ag_direct(ph, xg, r, p).wait_send()
             for r in (0, 1, 2, 3):
                 ag_forward(ph, xg, r, p).wait_send()
 
-    def rs_a(ph, n):
-        return remote(pbuf.at[ph, n, pl.ds(pl.multiple_of(64 * other, 64), 64), :], ra.at[ph, n], asend_sem.at[ph, n], arecv_sem.at[ph, n], partner)
+    def owner(half):
+        return pl.when(core == 1 - half)
+
+    def helper(half):
+        return pl.when(core == half)
+
+    def rs_a(ph, half, n):
+        return remote(pbuf.at[ph, half, n], ra.at[ph, n], asend_sem.at[ph, n], arecv_sem.at[ph, n], partner)
 
     def rs_b(ph, n, r):
         return remote(sb.at[ph, n, pl.ds(pl.multiple_of(16 * chips[r], 16), 16), :], rb.at[ph, r - 1, n], bsend_sem.at[ph, r, n], brecv_sem.at[ph, r, n], 2 * chips[r] + core)
 
-    def rs_put(ph, n, part):
-        pbuf[ph, n] = part.astype(BF16)
-        rs_a(ph, n).start()
-
-    def rs_pair(ph, n):
-        rs_a(ph, n).wait_recv()
-        own = pbuf[ph, n, pl.ds(pl.multiple_of(64 * core, 64), 64), :].astype(F32)
-        sb[ph, n] = (own + ra[ph, n].astype(F32)).astype(BF16)
-        for r in (3, 1, 2):
-            rs_b(ph, n, r).start()
+    def rs_put(ph, half, n, part):
+        pbuf[ph, half, n] = part.astype(BF16)
+
+        @helper(half)
+        def _():
+            rs_a(ph, half, n).start()
+
+    def rs_pairs(ph, half, pieces):
+        @owner(half)
+        def _():
+            for n in pieces:
+                rs_a(ph, half, n).wait_recv()
+                sb[ph, n] = (pbuf[ph, half, n].astype(F32) + ra[ph, n].astype(F32)).astype(BF16)
+                for r in (3, 1, 2):
+                    rs_b(ph, n, r).start()
 
     def rs_sum(ph, n):
         total = sb[ph, n, pl.ds(pl.multiple_of(16 * chip, 16), 16), :].astype(F32)
@@ -116,8 +135,11 @@
         return total
 
     def rs_finish(ph):
-        for n in range(NP):
-            rs_a(ph, n).wait_send()
+        for n in range(NQ):
+            for half in range(2):
+                @helper(half)
+                def _():
+                    rs_a(ph, half, n).wait_send()
             for r in (1, 2, 3):
                 rs_b(ph, n, r).wait_send()
 
@@ -137,9 +159,16 @@
             dst[my_rows, cols] = val.astype(BF16)
 
     gate_loads = []
-    for p in range(NP):
-        gate_loads.append(local(wg_hbm.at[pl.ds(p * CW, CW), :], wg.at[pl.ds(p * CW, CW), :], wsem.at[0, p]))
-        gate_loads.append(local(wu_hbm.at[pl.ds(p * CW, CW), :], wu.at[pl.ds(p * CW, CW), :], wsem.at[1, p]))
+    for p in range(NQ):
+        gate_loads.append(local(wg_hbm.at[pl.ds(p * CQ, CQ), :], wg.at[pl.ds(p * CQ, CQ), :], wsem.at[0, p]))
+        gate_loads.append(local(wu_hbm.at[pl.ds(p * CQ, CQ), :], wu.at[pl.ds(p * CQ, CQ), :], wsem.at[1, p]))
+
+    def start_mlp_rows():
+        for n in range(NQ):
+            cols = slice(n * CQ, n * CQ + CQ)
+            hb[:, cols] = (xv[:, cols].astype(F32) + rs_sum(0, n)).astype(BF16)
+        store_normed(hb, g2, xg2)
+        ag_start(1, xg2)
 
     def attention_phase(kc, vc, vt, wo, freqv, qs, kch, vch, bias, o_buf):
         loads = {
@@ -157,7 +186,9 @@
         barrier = pltpu.get_barrier_semaphore()
         for dev in (partner, 2 * flip1 + core, 2 * flip2 + core, 2 * flip3 + core):
             pl.semaphore_signal(barrier, inc=1, device_id={"tp": dev}, device_id_type=pl.DeviceIdType.MESH)
-        tok_lane = token_of_row(lax.broadcasted_iota(jnp.int32, (1, 128), 1))
+        lane1 = lax.broadcasted_iota(jnp.int32, (1, 128), 1)
+        tok_lane = token_of_row(lane1)
+        tok_half = [token_of_row(64 * half + lane1 % 64) for half in range(2)]
 
         def projection_phase(wq4, wqkv):
             wk_load = local(wk_hbm, wqkv.at[:, pl.ds(512, 128)], lsem.at[2])
@@ -205,15 +236,16 @@
                 vt[:, ks] = vc[ks, :].astype(F32).T.astype(BF16)
                 slot = i * KB + lax.broadcasted_iota(jnp.int32, (KB, 128), 0)
                 off = jnp.bitwise_and(slot - start, W - 1)
-                keep = jnp.where(off >= W - start, off, -1) > tok_lane
-                bias[ks, :] = jnp.where(keep, 0.0, -jnp.inf)
+                limit = jnp.where(off >= W - start, off, -1)
+                for half in range(2):
+                    bias[half, ks, :] = jnp.where(limit > tok_half[half], 0.0, -jnp.inf)
                 return carry
 
             loads["start"].wait()
             start = start_ref[0]
             for p in range(4):
                 split_heads(p)
-            for p in range(6):
+            for p in range(4):
                 flip_values(p, 0)
             loads["freq"].wait()
             tok_row = token_of_row(lax.broadcasted_iota(jnp.int32, (T, 128), 0))
@@ -233,8 +265,8 @@
                     ag_relay(0, xg1, p + 2)
                 if p + 4 < NP:
                     split_heads(p + 4)
-                if p < 2:
-                    flip_values(p + 6, 0)
+                if p < 4:
+                    flip_values(p + 4, 0)
                 ag_arrive(0, xg1, p)
                 cols = slice(p * CW, p * CW + CW)
                 acc = acc + jnp.dot(xg1[:, cols], wqkv[cols, :], preferred_element_type=F32)
@@ -246,7 +278,9 @@
                 return v * cos_t + swapped * sin_t
 
             for h in range(4):
-                qs[h * 128:h * 128 + 128, :] = rotate(acc[:, h * 128:h * 128 + 128]).astype(BF16)
+                turned = rotate(acc[:, h * 128:h * 128 + 128]).astype(BF16)
+                for half in range(2):
+                    qs[half, h * 64:h * 64 + 64, :] = turned[64 * half:64 * half + 64, :]
             kch[...] = rotate(acc[:, 512:640]).astype(BF16)
             v_new = acc[:, 640:768].astype(BF16)
             vch[...] = v_new
@@ -260,8 +294,8 @@
         loads["kc"].wait()
         factor = (128.0 ** -0.5) * 1.4426950408889634
 
-        def softmax_phase(s_buf):
-            queries = qs[...]
+        def softmax(half, s_buf, hook):
+            queries = qs[half]
             tops, masses = [], []
             for b in range(NKB + 1):
                 n = KB if b < NKB else T
@@ -269,11 +303,11 @@
                 keys = kc[ks, :] if b < NKB else kch[...]
                 st = lax.dot_general(keys, queries, (((1,), (1,)), ((), ())), preferred_element_type=F32)
                 if b < NKB:
-                    shift = bias[ks, :]
+                    shift = bias[half, ks, :]
                 else:
-                    shift = jnp.where(token_of_row(lax.broadcasted_iota(jnp.int32, (T, 128), 0)) <= tok_lane, 0.0, -jnp.inf)
+                    shift = jnp.where(token_of_row(lax.broadcasted_iota(jnp.int32, (T, 128), 0)) <= tok_half[half], 0.0, -jnp.inf)
                 top, mass = [], []
-                for g in range(4):
+                for g in range(2):
                     gs = slice(g * 128, g * 128 + 128)
                     part = st[:, gs] + shift
                     s_buf[ks, gs] = part
@@ -285,6 +319,8 @@
                     top.append(t)
                 tops.append(jnp.concatenate(top, axis=1))
                 masses.append(jnp.concatenate(mass, axis=1))
+                if b == 1:
+                    hook()
             best = functools.reduce(jnp.maximum, tops)
             scales = [jnp.exp2((t - best) * factor) for t in tops]
             total = sum(m * sc for m, sc in zip(masses, scales))
@@ -296,18 +332,29 @@
                 probs = (s_buf[ks, :] * (scales[b] * inv)).astype(BF16)
                 part = jnp.dot(vt[:, ks], probs, preferred_element_type=F32)
                 out = part if out is None else out + part
-            for g in range(4):
-                o_buf[:, g * 128:g * 128 + 128] = out[:, g * 128:g * 128 + 128].T.astype(BF16)
-
-        pl.run_scoped(softmax_phase, pltpu.VMEM((W + T, 512), F32))
-        loads["wo"].wait()
-        for n in range(NP):
-            cols = slice(n * CW, n * CW + CW)
-            rs_put(0, n, jnp.dot(o_buf[...], wo[:, cols], preferred_element_type=F32))
-            if n > 0:
-                rs_pair(0, n - 1)
-        rs_pair(0, NP - 1)
+            for g in range(2):
+                flipped = out[:, g * 128:g * 128 + 128].T.astype(BF16)
+                for j in range(2):
+                    h = 2 * g + j
+                    o_buf[half, :, h * 128:h * 128 + 128] = flipped[64 * j:64 * j + 64, :]
+
+        def project_out(half):
+            for n in range(NQ):
+                cols = slice(n * CQ, n * CQ + CQ)
+                rs_put(0, half, n, jnp.dot(o_buf[half], wo[:, cols], preferred_element_type=F32))
+
+        def softmax_phase(s_buf):
+            softmax(0, s_buf, lambda: None)
+            loads["wo"].wait()
+            project_out(0)
+            rs_pairs(0, 0, range(NQ // 2))
+            softmax(1, s_buf, lambda: rs_pairs(0, 0, range(NQ // 2, NQ)))
+
+        pl.run_scoped(softmax_phase, pltpu.VMEM((W + T, 256), F32))
+        project_out(1)
+        rs_pairs(0, 1, range(NQ))
         loads["g2"].wait()
+        owner(0)(start_mlp_rows)
 
         chunk = jnp.concatenate([kch[...], vch[...]], axis=1)
 
@@ -332,64 +379,91 @@
         pltpu.VMEM((128, W + T), BF16),
         pltpu.VMEM((512, D), BF16),
         pltpu.VMEM((8, 128), F32),
-        pltpu.VMEM((512, 128), BF16),
+        pltpu.VMEM((2, 256, 128), BF16),
         pltpu.VMEM((T, 128), BF16),
         pltpu.VMEM((T, 128), BF16),
-        pltpu.VMEM((W, 128), F32),
-        pltpu.VMEM((T, 512), BF16),
+        pltpu.VMEM((2, W, 128), F32),
+        pltpu.VMEM((2, 64, 512), BF16),
     )
 
     def mlp_phase(wd, acc_g, acc_u, u_buf):
-        down_loads = [local(wd_hbm.at[:, pl.ds(n * CW, CW)], wd.at[:, pl.ds(n * CW, CW)], dsem.at[n]) for n in range(NP)]
+        down_loads = [local(wd_hbm.at[:, pl.ds(n * CQ, CQ)], wd.at[:, pl.ds(n * CQ, CQ)], dsem.at[n]) for n in range(NQ)]
         for ld in down_loads:
             ld.start()
-        for n in range(NP):
-            cols = slice(n * CW, n * CW + CW)
-            hb[:, cols] = (xv[:, cols].astype(F32) + rs_sum(0, n)).astype(BF16)
-        store_normed(hb, g2, xg2)
-        ag_start(1, xg2)
-        ag_finish(0, xg1)
-        rs_finish(0)
-        ag_relay(1, xg2, 0)
-        ag_relay(1, xg2, 1)
-        for p in range(NP):
-            if p + 2 < NP:
-                ag_relay(1, xg2, p + 2)
-            gate_loads[2 * p].wait()
-            gate_loads[2 * p + 1].wait()
-            ag_arrive(1, xg2, p)
-            rows = slice(p * CW, p * CW + CW)
-            m = xg2[:, rows]
+
+        def relay(half, p):
+            @owner(half)
+            def _():
+                ag_relay(1, xg2, p)
+
+        def arrive(half, p):
+            @helper(half)
+            def _():
+                ag_arrive(1, xg2, p)
+
+        def gate_up(half, p):
+            if half == 0:
+                gate_loads[2 * p].wait()
+                gate_loads[2 * p + 1].wait()
+            arrive(half, p)
+            rows = slice(p * CQ, p * CQ + CQ)
+            m = xg2[64 * half:64 * half + 64, rows]
             gate = jnp.dot(m, wg[rows, :], preferred_element_type=F32)
             up = jnp.dot(m, wu[rows, :], preferred_element_type=F32)
             if p == 0:
                 acc_g[...] = gate
                 acc_u[...] = up
-            elif p + 1 < NP:
+            elif p + 1 < NQ:
                 acc_g[...] += gate
                 acc_u[...] += up
             else:
                 gate = acc_g[...] + gate
                 u_buf[...] = (gate / (1.0 + jnp.exp(-gate)) * (acc_u[...] + up)).astype(BF16)
-        for n in range(NP):
-            cols = slice(n * CW, n * CW + CW)
-            down_loads[n].wait()
-            rs_put(1, n, jnp.dot(u_buf[...], wd[:, cols], preferred_element_type=F32))
+
+        def down(half, n):
+            cols = slice(n * CQ, n * CQ + CQ)
+            if half == 0:
+                down_loads[n].wait()
+            rs_put(1, half, n, jnp.dot(u_buf[...], wd[:, cols], preferred_element_type=F32))
+
+        for p in range(AHEAD):
+            relay(0, p)
+        for p in range(NQ):
+            if p + AHEAD < NQ:
+                relay(0, p + AHEAD)
+            gate_up(0, p)
+            if p == NQ // 4:
+                owner(1)(start_mlp_rows)
+        for n in range(NQ):
+            down(0, n)
             if n > 0:
-                rs_pair(1, n - 1)
-        rs_pair(1, NP - 1)
+                rs_pairs(1, 0, [n - 1])
+            if n + 1 < NQ:
+                relay(1, n)
+        rs_pairs(1, 0, [NQ - 1])
+        for p in range(NQ):
+            if p == 0:
+                relay(1, NQ - 1)
+            gate_up(1, p)
+        for n in range(NQ):
+            down(1, n)
+            if n > 0:
+                rs_pairs(1, 1, [n - 1])
+        rs_pairs(1, 1, [NQ - 1])
+        ag_finish(0, xg1)
+        rs_finish(0)
         ag_finish(1, xg2)
-        for n in range(NP):
-            cols = slice(n * CW, n * CW + CW)
+        for n in range(NQ):
+            cols = slice(n * CQ, n * CQ + CQ)
             xo_ref[:, cols] = (hb[:, cols].astype(F32) + rs_sum(1, n)).astype(BF16)
         rs_finish(1)
 
     pl.run_scoped(
         mlp_phase,
         pltpu.VMEM((FF, D), BF16),
-        pltpu.VMEM((T, FF), F32),
-        pltpu.VMEM((T, FF), F32),
-        pltpu.VMEM((T, FF), BF16),
+        pltpu.VMEM((64, FF), F32),
+        pltpu.VMEM((64, FF), F32),
+        pltpu.VMEM((64, FF), BF16),
     )
 
 
@@ -422,10 +496,10 @@
                 pltpu.VMEM((D, FF), BF16),
                 pltpu.VMEM((T, D), BF16),
                 pltpu.VMEM((T, D), BF16),
-                pltpu.VMEM((2, NP, T, CW), BF16),
-                pltpu.VMEM((2, NP, 64, CW), BF16),
-                pltpu.VMEM((2, NP, 64, CW), BF16),
-                pltpu.VMEM((2, 3, NP, 16, CW), BF16),
+                pltpu.VMEM((2, 2, NQ, 64, CQ), BF16),
+                pltpu.VMEM((2, NQ, 64, CQ), BF16),
+                pltpu.VMEM((2, NQ, 64, CQ), BF16),
+                pltpu.VMEM((2, 3, NQ, 16, CQ), BF16),
                 pltpu.VMEM((16, D), BF16),
                 dma((10,)),
                 dma((2, NP)),

time: 53 us -> 57.2 us (1.079)
  Pallas kernels: 49 us -> 53.2 us
    pallas_call x1, Pallas kernels: 49 us -> 53.2 us  [local_layer(): pl.pallas_call(layer_kernel, out_shape=(pltpu.VMEM((16, D), BF16), pltpu....]
where the time goes in v4:
time: 57.2 us; the launch traced here: 57.1 us
  Pallas kernels  53.2 us (93%)
  local copies, waits for them, and re-layouts  2.6 us (5%)
  between operations  1.29 us (2%)
    pallas_call x1, Pallas kernels, local_layer(): pl.pallas_call(layer_kernel, out_shape=(pltpu.VMEM((16, D), BF16), pltpu....  53.2 us
    unnamed x3, local copies, waits for them, and re-layouts  2.6 us

profile of v4, /device:TPU:0, one launch (start us, length us, event | category | flops | bytes accessed | tf_op | source)
XLA Modules:
  0.0 57.1 jit_solution(1452043861440227996)
XLA Ops:
  1.3 53.2 %layer.1 = (bf16[16,4096]{1,0:T(8,128)(2,1)S(1)}, bf16[4096,128]{1,0:T(8,128)(2,1)S(1)}, bf16[4096,128]{1,0:T(8,128)(2,1)S(1)}) custom-call(s32[1]{0:T(128)S(6)} %copy.23.start_hbm, bf16[16,4096]{1,0:T(8,128)(2,1)} %bitcast.21, f32[8,128]{1,0:T(8,128)} %constant.2.clone.freq_hbm, bf16[4096,128]{1,0:T(8,128)(2,1)} %bitcast.17, bf16[4096,128]{1,0:T(8,128)(2,1)} %bitcast.18, ...), custom_call_target="tpu_custom_call" | custom-call | tf_op jit(solution)/shard_map/layer/pallas_call | solution.py:485
  54.5 0.7 %copy.20 = bf16[1,16,4096]{2,1,0:T(8,128)(2,1)} copy(bf16[1,16,4096]{2,1,0:T(8,128)(2,1)S(1)} %bitcast.14) | data formatting | bytes 262144
  55.2 1.0 %copy.21 = bf16[1,4096,1,128]{3,1,2,0:T(8,128)(2,1)} copy(bf16[1,4096,1,128]{3,1,2,0:T(8,128)(2,1)S(1)} %bitcast.13) | data formatting | bytes 2097152
  56.2 1.0 %copy.22 = bf16[1,4096,1,128]{3,1,2,0:T(8,128)(2,1)} copy(bf16[1,4096,1,128]{3,1,2,0:T(8,128)(2,1)S(1)} %bitcast.12) | data formatting | bytes 2097152

commit v5 on v3

--- a/solution.py
+++ b/solution.py
@@ -17,8 +17,13 @@
 FF = 1792
 W = 4096
 NP = 8
+CW = D // NP
+GATHER = [(512 * p, 512) for p in range(7)] + [(3584, 256), (3840, 256)]
+SCATTER = [(512 * p, 512) for p in range(8)]
+NA = len(GATHER)
+NR = len(SCATTER)
+LAG = 3
 VMEM_LIMIT = 64000000
-CW = D // NP
 KB = 512
 NKB = W // KB
 
@@ -54,23 +59,23 @@
         return pltpu.make_async_copy(src, dst, sem)
 
     def ag_direct(ph, xg, r, p):
-        cols = pl.ds(p * CW, CW)
+        cols = pl.ds(*GATHER[p])
         return remote(xg.at[my_rows, cols], xg.at[my_rows, cols], send_sem.at[ph, r, p], recv_sem.at[ph, r, p], 2 * chips[r] + core)
 
     def ag_direct_in(ph, xg, r, p):
-        ref = xg.at[rows_of(core, chips[r]), pl.ds(p * CW, CW)]
+        ref = xg.at[rows_of(core, chips[r]), pl.ds(*GATHER[p])]
         return remote(ref, ref, send_sem.at[ph, r, p], recv_sem.at[ph, r, p], 2 * chips[r] + core)
 
     def ag_forward(ph, xg, r, p):
-        ref = xg.at[rows_of(core, chips[r]), pl.ds(p * CW, CW)]
+        ref = xg.at[rows_of(core, chips[r]), pl.ds(*GATHER[p])]
         return remote(ref, ref, fsend_sem.at[ph, r, p], frecv_sem.at[ph, r, p], partner)
 
     def ag_forward_in(ph, xg, r, p):
-        ref = xg.at[rows_of(other, chips[r]), pl.ds(p * CW, CW)]
+        ref = xg.at[rows_of(other, chips[r]), pl.ds(*GATHER[p])]
         return remote(ref, ref, fsend_sem.at[ph, r, p], frecv_sem.at[ph, r, p], partner)
 
     def ag_start(ph, xg):
-        for p in range(NP):
+        for p in range(NA):
             for r in (3, 1, 2):
                 ag_direct(ph, xg, r, p).start()
             ag_forward(ph, xg, 0, p).start()
@@ -85,38 +90,53 @@
             ag_forward_in(ph, xg, r, p).wait_recv()
 
     def ag_finish(ph, xg):
-        for p in range(NP):
+        for p in range(NA):
             for r in (1, 2, 3):
                 ag_direct(ph, xg, r, p).wait_send()
             for r in (0, 1, 2, 3):
                 ag_forward(ph, xg, r, p).wait_send()
 
     def rs_a(ph, n):
-        return remote(pbuf.at[ph, n, pl.ds(pl.multiple_of(64 * other, 64), 64), :], ra.at[ph, n], asend_sem.at[ph, n], arecv_sem.at[ph, n], partner)
+        cols = pl.ds(*SCATTER[n])
+        return remote(pbuf.at[ph, pl.ds(pl.multiple_of(64 * other, 64), 64), cols], ra.at[ph, :, cols], asend_sem.at[ph, n], arecv_sem.at[ph, n], partner)
 
     def rs_b(ph, n, r):
-        return remote(sb.at[ph, n, pl.ds(pl.multiple_of(16 * chips[r], 16), 16), :], rb.at[ph, r - 1, n], bsend_sem.at[ph, r, n], brecv_sem.at[ph, r, n], 2 * chips[r] + core)
+        cols = pl.ds(*SCATTER[n])
+        return remote(sb.at[ph, pl.ds(pl.multiple_of(16 * chips[r], 16), 16), cols], rb.at[ph, r - 1, :, cols], bsend_sem.at[ph, r, n], brecv_sem.at[ph, r, n], 2 * chips[r] + core)
 
     def rs_put(ph, n, part):
-        pbuf[ph, n] = part.astype(BF16)
+        pbuf[ph, :, pl.ds(*SCATTER[n])] = part.astype(BF16)
         rs_a(ph, n).start()
 
     def rs_pair(ph, n):
+        cols = pl.ds(*SCATTER[n])
         rs_a(ph, n).wait_recv()
-        own = pbuf[ph, n, pl.ds(pl.multiple_of(64 * core, 64), 64), :].astype(F32)
-        sb[ph, n] = (own + ra[ph, n].astype(F32)).astype(BF16)
+        own = pbuf[ph, pl.ds(pl.multiple_of(64 * core, 64), 64), cols].astype(F32)
+        sb[ph, :, cols] = (own + ra[ph, :, cols].astype(F32)).astype(BF16)
         for r in (3, 1, 2):
             rs_b(ph, n, r).start()
 
+    def rs_all(ph, product, group):
+        for n in range(0, NR, group):
+            part = product(n, pl.ds(SCATTER[n][0], group * CW))
+            for k in range(group):
+                rs_put(ph, n + k, part[:, k * CW:k * CW + CW])
+            for k in range(n - LAG, n - LAG + group):
+                if k >= 0:
+                    rs_pair(ph, k)
+        for n in range(NR - LAG, NR):
+            rs_pair(ph, n)
+
     def rs_sum(ph, n):
-        total = sb[ph, n, pl.ds(pl.multiple_of(16 * chip, 16), 16), :].astype(F32)
+        cols = pl.ds(*SCATTER[n])
+        total = sb[ph, pl.ds(pl.multiple_of(16 * chip, 16), 16), cols].astype(F32)
         for r in (1, 2, 3):
             rs_b(ph, n, r).wait_recv()
-            total = total + rb[ph, r - 1, n].astype(F32)
+            total = total + rb[ph, r - 1, :, cols].astype(F32)
         return total
 
     def rs_finish(ph):
-        for n in range(NP):
+        for n in range(NR):
             rs_a(ph, n).wait_send()
             for r in (1, 2, 3):
                 rs_b(ph, n, r).wait_send()
@@ -137,11 +157,12 @@
             dst[my_rows, cols] = val.astype(BF16)
 
     gate_loads = []
-    for p in range(NP):
-        gate_loads.append(local(wg_hbm.at[pl.ds(p * CW, CW), :], wg.at[pl.ds(p * CW, CW), :], wsem.at[0, p]))
-        gate_loads.append(local(wu_hbm.at[pl.ds(p * CW, CW), :], wu.at[pl.ds(p * CW, CW), :], wsem.at[1, p]))
-
-    def attention_phase(kc, vc, vt, wo, freqv, qs, kch, vch, bias, o_buf):
+    for p in range(NA):
+        rows = pl.ds(*GATHER[p])
+        gate_loads.append(local(wg_hbm.at[rows, :], wg.at[rows, :], wsem.at[0, p]))
+        gate_loads.append(local(wu_hbm.at[rows, :], wu.at[rows, :], wsem.at[1, p]))
+
+    def attention_phase(kc, vc, vt, wo, freqv, qt, kch, vch, bias, o_buf):
         loads = {
             "x": local(x_hbm, xv, lsem.at[0]),
             "g1": local(g1_hbm, g1, lsem.at[1]),
@@ -228,15 +249,15 @@
             acc = jnp.zeros((T, 768), F32)
             ag_relay(0, xg1, 0)
             ag_relay(0, xg1, 1)
-            for p in range(NP):
-                if p + 2 < NP:
+            for p in range(NA):
+                if p + 2 < NA:
                     ag_relay(0, xg1, p + 2)
                 if p + 4 < NP:
                     split_heads(p + 4)
                 if p < 2:
                     flip_values(p + 6, 0)
                 ag_arrive(0, xg1, p)
-                cols = slice(p * CW, p * CW + CW)
+                cols = pl.ds(*GATHER[p])
                 acc = acc + jnp.dot(xg1[:, cols], wqkv[cols, :], preferred_element_type=F32)
             for ld in gate_loads:
                 ld.start()
@@ -246,7 +267,7 @@
                 return v * cos_t + swapped * sin_t
 
             for h in range(4):
-                qs[h * 128:h * 128 + 128, :] = rotate(acc[:, h * 128:h * 128 + 128]).astype(BF16)
+                qt[:, h * 128:h * 128 + 128] = rotate(acc[:, h * 128:h * 128 + 128]).T.astype(BF16)
             kch[...] = rotate(acc[:, 512:640]).astype(BF16)
             v_new = acc[:, 640:768].astype(BF16)
             vch[...] = v_new
@@ -260,40 +281,47 @@
         loads["kc"].wait()
         factor = (128.0 ** -0.5) * 1.4426950408889634
 
-        def softmax_phase(s_buf):
-            queries = qs[...]
+        def softmax_phase(e_buf):
+            queries = qt[...]
             tops, masses = [], []
             for b in range(NKB + 1):
-                n = KB if b < NKB else T
-                ks = slice(b * KB, b * KB + n)
-                keys = kc[ks, :] if b < NKB else kch[...]
-                st = lax.dot_general(keys, queries, (((1,), (1,)), ((), ())), preferred_element_type=F32)
-                if b < NKB:
-                    shift = bias[ks, :]
-                else:
-                    shift = jnp.where(token_of_row(lax.broadcasted_iota(jnp.int32, (T, 128), 0)) <= tok_lane, 0.0, -jnp.inf)
-                top, mass = [], []
-                for g in range(4):
-                    gs = slice(g * 128, g * 128 + 128)
-                    part = st[:, gs] + shift
-                    s_buf[ks, gs] = part
-                    t = jnp.max(jnp.max(part.reshape(n // 8, 8, 128), axis=0), axis=0, keepdims=True)
-                    t = jnp.maximum(t, jnp.finfo(F32).min)
-                    e = jnp.exp2((s_buf[ks, gs] - t) * factor)
-                    s_buf[ks, gs] = e
-                    mass.append(jnp.sum(jnp.sum(e.reshape(n // 8, 8, 128), axis=0), axis=0, keepdims=True))
-                    top.append(t)
-                tops.append(jnp.concatenate(top, axis=1))
-                masses.append(jnp.concatenate(mass, axis=1))
-            best = functools.reduce(jnp.maximum, tops)
-            scales = [jnp.exp2((t - best) * factor) for t in tops]
-            total = sum(m * sc for m, sc in zip(masses, scales))
-            inv = 1.0 / total
+                keys = kc[b * KB:b * KB + KB, :] if b < NKB else kch[...]
+                scores = jnp.dot(keys, queries, preferred_element_type=F32)
+                for i in range(KB // 128 if b < NKB else 1):
+                    ks = slice(b * KB + i * 128, b * KB + i * 128 + 128)
+                    if b < NKB:
+                        shift = bias[ks, :]
+                    else:
+                        shift = jnp.where(token_of_row(lax.broadcasted_iota(jnp.int32, (T, 128), 0)) <= tok_lane, 0.0, -jnp.inf)
+                    top, mass = [], []
+                    for g in range(4):
+                        gs = slice(g * 128, g * 128 + 128)
+                        part = (scores[i * 128:i * 128 + 128, gs] + shift).reshape(16, 8, 128)
+                        t = jnp.maximum(jnp.max(part, axis=0), jnp.finfo(F32).min)
+                        e = jnp.exp2((part - t[None]) * factor)
+                        e_buf[ks, gs] = e.reshape(128, 128)
+                        mass.append(jnp.sum(e, axis=0))
+                        top.append(t)
+                    tops.append(top)
+                    masses.append(mass)
+            blocks = len(tops)
+            weights = []
+            for g in range(4):
+                best = jnp.max(functools.reduce(jnp.maximum, [tops[b][g] for b in range(blocks)]), axis=0, keepdims=True)
+                scales = [jnp.exp2((tops[b][g] - best) * factor) for b in range(blocks)]
+                total = functools.reduce(jnp.add, [masses[b][g] * scales[b] for b in range(blocks)])
+                inv = 1.0 / jnp.sum(total, axis=0, keepdims=True)
+                weights.append([sc * inv for sc in scales])
             out = None
             for b in range(NKB + 1):
                 n = KB if b < NKB else T
                 ks = slice(b * KB, b * KB + n)
-                probs = (s_buf[ks, :] * (scales[b] * inv)).astype(BF16)
+                rows = []
+                for i in range(n // 128):
+                    r0 = b * KB + i * 128
+                    cols = [(e_buf[r0:r0 + 128, g * 128:g * 128 + 128].reshape(16, 8, 128) * weights[g][b * (KB // 128) + i][None]).reshape(128, 128) for g in range(4)]
+                    rows.append(jnp.concatenate(cols, axis=1))
+                probs = jnp.concatenate(rows, axis=0).astype(BF16)
                 part = jnp.dot(vt[:, ks], probs, preferred_element_type=F32)
                 out = part if out is None else out + part
             for g in range(4):
@@ -301,12 +329,7 @@
 
         pl.run_scoped(softmax_phase, pltpu.VMEM((W + T, 512), F32))
         loads["wo"].wait()
-        for n in range(NP):
-            cols = slice(n * CW, n * CW + CW)
-            rs_put(0, n, jnp.dot(o_buf[...], wo[:, cols], preferred_element_type=F32))
-            if n > 0:
-                rs_pair(0, n - 1)
-        rs_pair(0, NP - 1)
+        rs_all(0, lambda n, cols: jnp.dot(o_buf[...], wo[:, cols], preferred_element_type=F32), 2)
         loads["g2"].wait()
 
         chunk = jnp.concatenate([kch[...], vch[...]], axis=1)
@@ -332,7 +355,7 @@
         pltpu.VMEM((128, W + T), BF16),
         pltpu.VMEM((512, D), BF16),
         pltpu.VMEM((8, 128), F32),
-        pltpu.VMEM((512, 128), BF16),
+        pltpu.VMEM((128, 512), BF16),
         pltpu.VMEM((T, 128), BF16),
         pltpu.VMEM((T, 128), BF16),
         pltpu.VMEM((W, 128), F32),
@@ -343,8 +366,8 @@
         down_loads = [local(wd_hbm.at[:, pl.ds(n * CW, CW)], wd.at[:, pl.ds(n * CW, CW)], dsem.at[n]) for n in range(NP)]
         for ld in down_loads:
             ld.start()
-        for n in range(NP):
-            cols = slice(n * CW, n * CW + CW)
+        for n in range(NR):
+            cols = pl.ds(*SCATTER[n])
             hb[:, cols] = (xv[:, cols].astype(F32) + rs_sum(0, n)).astype(BF16)
         store_normed(hb, g2, xg2)
         ag_start(1, xg2)
@@ -352,35 +375,33 @@
         rs_finish(0)
         ag_relay(1, xg2, 0)
         ag_relay(1, xg2, 1)
-        for p in range(NP):
-            if p + 2 < NP:
+        for p in range(NA):
+            if p + 2 < NA:
                 ag_relay(1, xg2, p + 2)
             gate_loads[2 * p].wait()
             gate_loads[2 * p + 1].wait()
             ag_arrive(1, xg2, p)
-            rows = slice(p * CW, p * CW + CW)
+            rows = pl.ds(*GATHER[p])
             m = xg2[:, rows]
             gate = jnp.dot(m, wg[rows, :], preferred_element_type=F32)
             up = jnp.dot(m, wu[rows, :], preferred_element_type=F32)
             if p == 0:
                 acc_g[...] = gate
                 acc_u[...] = up
-            elif p + 1 < NP:
+            elif p + 1 < NA:
                 acc_g[...] += gate
                 acc_u[...] += up
             else:
                 gate = acc_g[...] + gate
                 u_buf[...] = (gate / (1.0 + jnp.exp(-gate)) * (acc_u[...] + up)).astype(BF16)
-        for n in range(NP):
-            cols = slice(n * CW, n * CW + CW)
+        def down(n, cols):
             down_loads[n].wait()
-            rs_put(1, n, jnp.dot(u_buf[...], wd[:, cols], preferred_element_type=F32))
-            if n > 0:
-                rs_pair(1, n - 1)
-        rs_pair(1, NP - 1)
+            return jnp.dot(u_buf[...], wd[:, cols], preferred_element_type=F32)
+
+        rs_all(1, down, 1)
         ag_finish(1, xg2)
-        for n in range(NP):
-            cols = slice(n * CW, n * CW + CW)
+        for n in range(NR):
+            cols = pl.ds(*SCATTER[n])
             xo_ref[:, cols] = (hb[:, cols].astype(F32) + rs_sum(1, n)).astype(BF16)
         rs_finish(1)
 
@@ -391,6 +412,14 @@
         pltpu.VMEM((T, FF), F32),
         pltpu.VMEM((T, FF), BF16),
     )
+
+
+def write_kernel(x_ref, k_ref, v_ref, xo_hbm, ko_hbm, vo_hbm, sem):
+    copies = [pltpu.make_async_copy(src, dst, sem.at[i]) for i, (src, dst) in enumerate(((k_ref, ko_hbm), (v_ref, vo_hbm), (x_ref, xo_hbm)))]
+    for copy in copies:
+        copy.start()
+    for copy in copies:
+        copy.wait()
 
 
 def solution(mesh):
@@ -408,10 +437,10 @@
         dma = pltpu.SemaphoreType.DMA
         kc2 = k_cache.reshape(W, 128)
         vc2 = v_cache.reshape(W, 128)
-        x_out, k_new, v_new = pl.pallas_call(
+        results = pl.pallas_call(
             layer_kernel,
             out_shape=(pltpu.VMEM((16, D), BF16), pltpu.VMEM((W, 128), BF16), pltpu.VMEM((W, 128), BF16)),
-            in_specs=[any_spec] * 14,
+            in_specs=[pl.BlockSpec(memory_space=pltpu.HBM)] + [any_spec] * 13,
             out_specs=(vmem_spec, vmem_spec, vmem_spec),
             scratch_shapes=[
                 pltpu.SMEM((1,), jnp.int32),
@@ -422,22 +451,22 @@
                 pltpu.VMEM((D, FF), BF16),
                 pltpu.VMEM((T, D), BF16),
                 pltpu.VMEM((T, D), BF16),
-                pltpu.VMEM((2, NP, T, CW), BF16),
-                pltpu.VMEM((2, NP, 64, CW), BF16),
-                pltpu.VMEM((2, NP, 64, CW), BF16),
-                pltpu.VMEM((2, 3, NP, 16, CW), BF16),
+                pltpu.VMEM((2, T, D), BF16),
+                pltpu.VMEM((2, 64, D), BF16),
+                pltpu.VMEM((2, 64, D), BF16),
+                pltpu.VMEM((2, 3, 16, D), BF16),
                 pltpu.VMEM((16, D), BF16),
                 dma((10,)),
-                dma((2, NP)),
+                dma((2, NA)),
                 dma((NP,)),
-                dma((2, 4, NP)),
-                dma((2, 4, NP)),
-                dma((2, 4, NP)),
-                dma((2, 4, NP)),
-                dma((2, NP)),
-                dma((2, NP)),
-                dma((2, 4, NP)),
-                dma((2, 4, NP)),
+                dma((2, 4, NA)),
+                dma((2, 4, NA)),
+                dma((2, 4, NA)),
+                dma((2, 4, NA)),
+                dma((2, NR)),
+                dma((2, NR)),
+                dma((2, 4, NR)),
+                dma((2, 4, NR)),
             ],
             compiler_params=pltpu.CompilerParams(collective_id=0, has_side_effects=True, vmem_limit_bytes=VMEM_LIMIT),
             name="layer",
@@ -445,6 +474,15 @@
             start_pos, x_in.reshape(16, D), freq, kc2, vc2, attn_gain.reshape(32, 128), w_query.reshape(4 * D, 128),
             w_key.reshape(D, 128), w_value.reshape(D, 128), w_out.reshape(512, D), mlp_gain.reshape(32, 128), w_gate, w_up, w_down,
         )
+        x_out, k_new, v_new = pl.pallas_call(
+            write_kernel,
+            out_shape=(jax.ShapeDtypeStruct((16, D), BF16), jax.ShapeDtypeStruct((W, 128), BF16), jax.ShapeDtypeStruct((W, 128), BF16)),
+            in_specs=[vmem_spec] * 3,
+            out_specs=(pl.BlockSpec(memory_space=pltpu.HBM),) * 3,
+            scratch_shapes=[dma((3,))],
+            compiler_params=pltpu.CompilerParams(vmem_limit_bytes=1 << 20),
+            name="write",
+        )(*[pltpu.with_memory_space_constraint(r, pltpu.VMEM) for r in results])
         return x_out.reshape(x_in.shape), k_new.reshape(k_cache.shape), v_new.reshape(v_cache.shape)
 
     return jax.shard_map(local_layer, mesh=mesh, in_specs=in_specs, out_specs=out_specs, check_vma=False)

time: 53 us -> 53.2 us (level)
  Pallas kernels: 49 us -> 51.6 us
  local copies, waits for them, and re-layouts: 2.6 us -> 0 us
    unnamed x3 -> x0, local copies, waits for them, and re-layouts: 2.6 us -> none
    pallas_call x0 -> x1, Pallas kernels: none -> 1.37 us  [local_layer(): pl.pallas_call(write_kernel, out_shape=(jax.ShapeDtypeStruct((16, D), BF1...]
    pallas_call x1, Pallas kernels: 49 us -> 50.3 us  [local_layer(): pl.pallas_call(layer_kernel, out_shape=(pltpu.VMEM((16, D), BF16), pltpu....]
where the time goes in v5:
time: 53.2 us; the launch traced here: 53.1 us
  Pallas kernels  51.6 us (97%)
  between operations  1.45 us (3%)
    pallas_call x1, Pallas kernels, local_layer(): pl.pallas_call(layer_kernel, out_shape=(pltpu.VMEM((16, D), BF16), pltpu....  50.3 us
    pallas_call x1, Pallas kernels, local_layer(): pl.pallas_call(write_kernel, out_shape=(jax.ShapeDtypeStruct((16, D), BF1...  1.37 us

profile of v5, /device:TPU:0, one launch (start us, length us, event | category | flops | bytes accessed | tf_op | source)
XLA Modules:
  0.0 53.1 jit_solution(9221408811462660566)
XLA Ops:
  1.3 50.3 %layer.1 = (bf16[16,4096]{1,0:T(8,128)(2,1)S(1)}, bf16[4096,128]{1,0:T(8,128)(2,1)S(1)}, bf16[4096,128]{1,0:T(8,128)(2,1)S(1)}) custom-call(s32[1]{0:T(128)S(6)} %copy.17.start_hbm, bf16[16,4096]{1,0:T(8,128)(2,1)} %bitcast.18, f32[8,128]{1,0:T(8,128)} %constant.2.clone.freq_hbm, bf16[4096,128]{1,0:T(8,128)(2,1)} %bitcast.14, bf16[4096,128]{1,0:T(8,128)(2,1)} %bitcast.15, ...), custom_call_target="tpu_custom_call" | custom-call | tf_op jit(solution)/shard_map/layer/pallas_call | solution.py:440
  51.6 1.4 %write.1 = (bf16[16,4096]{1,0:T(8,128)(2,1)}, bf16[4096,128]{1,0:T(8,128)(2,1)}, bf16[4096,128]{1,0:T(8,128)(2,1)}) custom-call(bf16[16,4096]{1,0:T(8,128)(2,1)S(1)} %get-tuple-element.9.x_ref, bf16[4096,128]{1,0:T(8,128)(2,1)S(1)} %get-tuple-element.10.k_ref, bf16[4096,128]{1,0:T(8,128)(2,1)S(1)} %get-tuple-element.11.v_ref), custom_call_target="tpu_custom_call" | custom-call | tf_op jit(solution)/shard_map/write/pallas_call | solution.py:477

commit v6 on v5

--- a/solution.py
+++ b/solution.py
@@ -22,7 +22,8 @@
 SCATTER = [(512 * p, 512) for p in range(8)]
 NA = len(GATHER)
 NR = len(SCATTER)
-LAG = 3
+LAG = 2
+VIA = 4
 VMEM_LIMIT = 64000000
 KB = 512
 NKB = W // KB
@@ -36,7 +37,7 @@
 
 def layer_kernel(start_hbm, x_hbm, freq_hbm, kc_hbm, vc_hbm, g1_hbm, wq_hbm, wk_hbm, wv_hbm, wo_hbm, g2_hbm, wg_hbm, wu_hbm, wd_hbm,
                  xo_ref, kn_ref, vn_ref,
-                 start_ref, xv, g1, g2, wg, wu, xg1, xg2, pbuf, ra, sb, rb, hb,
+                 start_ref, xv, g1, g2, wg, wu, xg1, xg2, pbuf, ra, sb, rb, tb, hb,
                  lsem, wsem, dsem, send_sem, recv_sem, fsend_sem, frecv_sem, asend_sem, arecv_sem, bsend_sem, brecv_sem):
     me = lax.axis_index("tp")
     core = me % 2
@@ -108,13 +109,33 @@
         pbuf[ph, :, pl.ds(*SCATTER[n])] = part.astype(BF16)
         rs_a(ph, n).start()
 
+    def rs_first(n):
+        return 1 + n % 2
+
+    def rs_transit(ph, n):
+        cols = pl.ds(*SCATTER[n])
+        src = sb.at[ph, pl.ds(pl.multiple_of(16 * chips[3], 16), 16), cols]
+        return remote(src, tb.at[ph, :, cols], bsend_sem.at[ph, 3, n], brecv_sem.at[ph, 3, n], 2 * chips[rs_first(n)] + core)
+
     def rs_pair(ph, n):
         cols = pl.ds(*SCATTER[n])
         rs_a(ph, n).wait_recv()
         own = pbuf[ph, pl.ds(pl.multiple_of(64 * core, 64), 64), cols].astype(F32)
         sb[ph, :, cols] = (own + ra[ph, :, cols].astype(F32)).astype(BF16)
-        for r in (3, 1, 2):
-            rs_b(ph, n, r).start()
+        if n < VIA:
+            rs_transit(ph, n).start()
+            rs_b(ph, n, rs_first(n)).start()
+        else:
+            for r in (3, 1, 2):
+                rs_b(ph, n, r).start()
+
+    def rs_cross(ph, n):
+        cols = pl.ds(*SCATTER[n])
+        second = 3 - rs_first(n)
+        rows = pl.ds(pl.multiple_of(16 * chips[second], 16), 16)
+        rs_transit(ph, n).wait_recv()
+        sb[ph, rows, cols] = (sb[ph, rows, cols].astype(F32) + tb[ph, :, cols].astype(F32)).astype(BF16)
+        rs_b(ph, n, second).start()
 
     def rs_all(ph, product, group):
         for n in range(0, NR, group):
@@ -126,11 +147,13 @@
                     rs_pair(ph, k)
         for n in range(NR - LAG, NR):
             rs_pair(ph, n)
+        for n in range(VIA):
+            rs_cross(ph, n)
 
     def rs_sum(ph, n):
         cols = pl.ds(*SCATTER[n])
         total = sb[ph, pl.ds(pl.multiple_of(16 * chip, 16), 16), cols].astype(F32)
-        for r in (1, 2, 3):
+        for r in (1, 2) if n < VIA else (1, 2, 3):
             rs_b(ph, n, r).wait_recv()
             total = total + rb[ph, r - 1, :, cols].astype(F32)
         return total
@@ -138,8 +161,9 @@
     def rs_finish(ph):
         for n in range(NR):
             rs_a(ph, n).wait_send()
-            for r in (1, 2, 3):
+            for r in (1, 2):
                 rs_b(ph, n, r).wait_send()
+            (rs_transit(ph, n) if n < VIA else rs_b(ph, n, 3)).wait_send()
 
     def normed(rows, gain):
         ms = jnp.zeros((16, 128), F32)
@@ -231,7 +255,7 @@
                 return carry
 
             loads["start"].wait()
-            start = start_ref[0]
+            start = start_ref[0:1, :]
             for p in range(4):
                 split_heads(p)
             for p in range(6):
@@ -345,7 +369,7 @@
             vn_ref[ks, :] = jnp.where(fresh, placed[:, 128:256], vc[ks, :].astype(F32)).astype(BF16)
             return carry
 
-        start = start_ref[0]
+        start = start_ref[0:1, :]
         lax.fori_loop(0, NKB, merge, 0)
 
     pl.run_scoped(
@@ -440,10 +464,10 @@
         results = pl.pallas_call(
             layer_kernel,
             out_shape=(pltpu.VMEM((16, D), BF16), pltpu.VMEM((W, 128), BF16), pltpu.VMEM((W, 128), BF16)),
-            in_specs=[pl.BlockSpec(memory_space=pltpu.HBM)] + [any_spec] * 13,
+            in_specs=[any_spec] * 14,
             out_specs=(vmem_spec, vmem_spec, vmem_spec),
             scratch_shapes=[
-                pltpu.SMEM((1,), jnp.int32),
+                pltpu.VMEM((8, 128), jnp.int32),
                 pltpu.VMEM((16, D), BF16),
                 pltpu.VMEM((32, 128), BF16),
                 pltpu.VMEM((32, 128), BF16),
@@ -455,6 +479,7 @@
                 pltpu.VMEM((2, 64, D), BF16),
                 pltpu.VMEM((2, 64, D), BF16),
                 pltpu.VMEM((2, 3, 16, D), BF16),
+                pltpu.VMEM((2, 16, VIA * CW), BF16),
                 pltpu.VMEM((16, D), BF16),
                 dma((10,)),
                 dma((2, NA)),
@@ -471,7 +496,7 @@
             compiler_params=pltpu.CompilerParams(collective_id=0, has_side_effects=True, vmem_limit_bytes=VMEM_LIMIT),
             name="layer",
         )(
-            start_pos, x_in.reshape(16, D), freq, kc2, vc2, attn_gain.reshape(32, 128), w_query.reshape(4 * D, 128),
+            jnp.broadcast_to(start_pos[:, None], (8, 128)), x_in.reshape(16, D), freq, kc2, vc2, attn_gain.reshape(32, 128), w_query.reshape(4 * D, 128),
             w_key.reshape(D, 128), w_value.reshape(D, 128), w_out.reshape(512, D), mlp_gain.reshape(32, 128), w_gate, w_up, w_down,
         )
         x_out, k_new, v_new = pl.pallas_call(

time: 53.2 us -> 52.7 us (level)
  Pallas kernels: 51.6 us -> 50.5 us
  local copies, waits for them, and re-layouts: 0 us -> 0.59 us
    pallas_call x1, Pallas kernels: 50.3 us -> 49.2 us  [local_layer(): pl.pallas_call(layer_kernel, out_shape=(pltpu.VMEM((16, D), BF16), pltpu....]
    broadcast_in_dim x0 -> x1, local copies, waits for them, and re-layouts: none -> 0.59 us  [local_layer(): jnp.broadcast_to(start_pos[:, None], (8, 128))]
where the time goes in v6:
time: 52.7 us; the launch traced here: 52.6 us
  Pallas kernels  50.5 us (96%)
  between operations  1.45 us (3%)
  local copies, waits for them, and re-layouts  0.59 us (1%)
    pallas_call x1, Pallas kernels, local_layer(): pl.pallas_call(layer_kernel, out_shape=(pltpu.VMEM((16, D), BF16), pltpu....  49.2 us
    pallas_call x1, Pallas kernels, local_layer(): pl.pallas_call(write_kernel, out_shape=(jax.ShapeDtypeStruct((16, D), BF1...  1.37 us

profile of v6, /device:TPU:0, one launch (start us, length us, event | category | flops | bytes accessed | tf_op | source)
XLA Modules:
  0.0 52.6 jit_solution(2390192712069136885)
XLA Ops:
  1.3 0.6 %broadcast_in_dim.9.start_hbm = s32[8,128]{1,0:T(8,128)} broadcast(s32[]{:T(128)} %bitcast.13), dimensions={} | broadcast | bytes 4100 | tf_op jit(solution)/shard_map/broadcast_in_dim | solution.py:499
  1.9 49.2 %layer.1 = (bf16[16,4096]{1,0:T(8,128)(2,1)S(1)}, bf16[4096,128]{1,0:T(8,128)(2,1)S(1)}, bf16[4096,128]{1,0:T(8,128)(2,1)S(1)}) custom-call(s32[8,128]{1,0:T(8,128)} %broadcast_in_dim.9.start_hbm, bf16[16,4096]{1,0:T(8,128)(2,1)} %bitcast.20, f32[8,128]{1,0:T(8,128)} %constant.2.clone.freq_hbm, bf16[4096,128]{1,0:T(8,128)(2,1)} %bitcast.16, ...), custom_call_target="tpu_custom_call" | custom-call | tf_op jit(solution)/shard_map/layer/pallas_call | solution.py:464
  51.0 1.4 %write.1 = (bf16[16,4096]{1,0:T(8,128)(2,1)}, bf16[4096,128]{1,0:T(8,128)(2,1)}, bf16[4096,128]{1,0:T(8,128)(2,1)}) custom-call(bf16[16,4096]{1,0:T(8,128)(2,1)S(1)} %get-tuple-element.9.x_ref, bf16[4096,128]{1,0:T(8,128)(2,1)S(1)} %get-tuple-element.10.k_ref, bf16[4096,128]{1,0:T(8,128)(2,1)S(1)} %get-tuple-element.11.v_ref), custom_call_target="tpu_custom_call" | custom-call | tf_op jit(solution)/shard_map/write/pallas_call | solution.py:502

commit v7 on v6

--- a/solution.py
+++ b/solution.py
@@ -21,9 +21,10 @@
 GATHER = [(512 * p, 512) for p in range(7)] + [(3584, 256), (3840, 256)]
 SCATTER = [(512 * p, 512) for p in range(8)]
 NA = len(GATHER)
+HAND = (6, 7, 8)
 NR = len(SCATTER)
 LAG = 2
-VIA = 4
+VIA = 6
 VMEM_LIMIT = 64000000
 KB = 512
 NKB = W // KB
@@ -38,7 +39,7 @@
 def layer_kernel(start_hbm, x_hbm, freq_hbm, kc_hbm, vc_hbm, g1_hbm, wq_hbm, wk_hbm, wv_hbm, wo_hbm, g2_hbm, wg_hbm, wu_hbm, wd_hbm,
                  xo_ref, kn_ref, vn_ref,
                  start_ref, xv, g1, g2, wg, wu, xg1, xg2, pbuf, ra, sb, rb, tb, hb,
-                 lsem, wsem, dsem, send_sem, recv_sem, fsend_sem, frecv_sem, asend_sem, arecv_sem, bsend_sem, brecv_sem):
+                 lsem, wsem, dsem, send_sem, recv_sem, fsend_sem, frecv_sem, asend_sem, arecv_sem, bsend_sem, brecv_sem, hsend_sem, hrecv_sem, gsend_sem, grecv_sem):
     me = lax.axis_index("tp")
     core = me % 2
     chip = me // 2
@@ -59,43 +60,103 @@
     def local(src, dst, sem):
         return pltpu.make_async_copy(src, dst, sem)
 
+    def piece(xg, c, r, p):
+        return xg.at[rows_of(c, chips[r]), pl.ds(*GATHER[p])]
+
     def ag_direct(ph, xg, r, p):
-        cols = pl.ds(*GATHER[p])
-        return remote(xg.at[my_rows, cols], xg.at[my_rows, cols], send_sem.at[ph, r, p], recv_sem.at[ph, r, p], 2 * chips[r] + core)
+        ref = piece(xg, core, 0, p)
+        return remote(ref, ref, send_sem.at[ph, r, p], recv_sem.at[ph, r, p], 2 * chips[r] + core)
 
     def ag_direct_in(ph, xg, r, p):
-        ref = xg.at[rows_of(core, chips[r]), pl.ds(*GATHER[p])]
+        ref = piece(xg, core, r, p)
         return remote(ref, ref, send_sem.at[ph, r, p], recv_sem.at[ph, r, p], 2 * chips[r] + core)
 
     def ag_forward(ph, xg, r, p):
-        ref = xg.at[rows_of(core, chips[r]), pl.ds(*GATHER[p])]
+        ref = piece(xg, core, r, p)
         return remote(ref, ref, fsend_sem.at[ph, r, p], frecv_sem.at[ph, r, p], partner)
 
     def ag_forward_in(ph, xg, r, p):
-        ref = xg.at[rows_of(other, chips[r]), pl.ds(*GATHER[p])]
+        ref = piece(xg, other, r, p)
         return remote(ref, ref, fsend_sem.at[ph, r, p], frecv_sem.at[ph, r, p], partner)
+
+    def ag_hand(ph, xg, r, p):
+        ref = piece(xg, 0, 0, p)
+        return remote(ref, ref, hsend_sem.at[ph, r, p - HAND[0]], hrecv_sem.at[ph, r, p - HAND[0]], 2 * chips[r] + 1)
+
+    def ag_hand_in(ph, xg, r, p):
+        ref = piece(xg, 0, r, p)
+        return remote(ref, ref, hsend_sem.at[ph, r, p - HAND[0]], hrecv_sem.at[ph, r, p - HAND[0]], 2 * chips[r] + 1)
+
+    def ag_hand_forward(ph, xg, r, p):
+        ref = piece(xg, 0, r, p)
+        return remote(ref, ref, gsend_sem.at[ph, r, p - HAND[0]], grecv_sem.at[ph, r, p - HAND[0]], partner)
+
+    def on_core(c):
+        return pl.when(core == c)
 
     def ag_start(ph, xg):
         for p in range(NA):
-            for r in (3, 1, 2):
-                ag_direct(ph, xg, r, p).start()
             ag_forward(ph, xg, 0, p).start()
+            if p not in HAND:
+                for r in (3, 1, 2):
+                    ag_direct(ph, xg, r, p).start()
+
+    def ag_start_last(ph, xg):
+        @on_core(1)
+        def _():
+            for p in HAND:
+                for r in (3, 1, 2):
+                    ag_direct(ph, xg, r, p).start()
+                ag_forward_in(ph, xg, 0, p).wait_recv()
+                for r in (3, 1, 2):
+                    ag_hand(ph, xg, r, p).start()
 
     def ag_relay(ph, xg, p):
-        for r in (1, 2, 3):
-            ag_direct_in(ph, xg, r, p).wait_recv()
-            ag_forward(ph, xg, r, p).start()
+        def pass_on():
+            for r in (1, 2, 3):
+                ag_direct_in(ph, xg, r, p).wait_recv()
+                ag_forward(ph, xg, r, p).start()
+
+        if p not in HAND:
+            pass_on()
+        else:
+            @on_core(1)
+            def _():
+                pass_on()
+                for r in (1, 2, 3):
+                    ag_hand_in(ph, xg, r, p).wait_recv()
+                    ag_hand_forward(ph, xg, r, p).start()
 
     def ag_arrive(ph, xg, p):
-        for r in (0, 1, 2, 3):
-            ag_forward_in(ph, xg, r, p).wait_recv()
+        def wait_all():
+            for r in (0, 1, 2, 3):
+                ag_forward_in(ph, xg, r, p).wait_recv()
+
+        if p not in HAND:
+            wait_all()
+        else:
+            @on_core(0)
+            def _():
+                wait_all()
+                for r in (1, 2, 3):
+                    ag_hand_forward(ph, xg, r, p).wait_recv()
 
     def ag_finish(ph, xg):
         for p in range(NA):
-            for r in (1, 2, 3):
-                ag_direct(ph, xg, r, p).wait_send()
-            for r in (0, 1, 2, 3):
-                ag_forward(ph, xg, r, p).wait_send()
+            ag_forward(ph, xg, 0, p).wait_send()
+            if p not in HAND:
+                for r in (1, 2, 3):
+                    ag_direct(ph, xg, r, p).wait_send()
+                    ag_forward(ph, xg, r, p).wait_send()
+
+        @on_core(1)
+        def _():
+            for p in HAND:
+                for r in (1, 2, 3):
+                    ag_direct(ph, xg, r, p).wait_send()
+                    ag_forward(ph, xg, r, p).wait_send()
+                    ag_hand(ph, xg, r, p).wait_send()
+                    ag_hand_forward(ph, xg, r, p).wait_send()
 
     def rs_a(ph, n):
         cols = pl.ds(*SCATTER[n])
@@ -255,7 +316,7 @@
                 return carry
 
             loads["start"].wait()
-            start = start_ref[0:1, :]
+            start = start_ref[0]
             for p in range(4):
                 split_heads(p)
             for p in range(6):
@@ -271,6 +332,7 @@
             wk_load.wait()
             wv_load.wait()
             acc = jnp.zeros((T, 768), F32)
+            ag_start_last(0, xg1)
             ag_relay(0, xg1, 0)
             ag_relay(0, xg1, 1)
             for p in range(NA):
@@ -369,7 +431,7 @@
             vn_ref[ks, :] = jnp.where(fresh, placed[:, 128:256], vc[ks, :].astype(F32)).astype(BF16)
             return carry
 
-        start = start_ref[0:1, :]
+        start = start_ref[0]
         lax.fori_loop(0, NKB, merge, 0)
 
     pl.run_scoped(
@@ -397,6 +459,7 @@
         ag_start(1, xg2)
         ag_finish(0, xg1)
         rs_finish(0)
+        ag_start_last(1, xg2)
         ag_relay(1, xg2, 0)
         ag_relay(1, xg2, 1)
         for p in range(NA):
@@ -467,7 +530,7 @@
             in_specs=[any_spec] * 14,
             out_specs=(vmem_spec, vmem_spec, vmem_spec),
             scratch_shapes=[
-                pltpu.VMEM((8, 128), jnp.int32),
+                pltpu.SMEM((1,), jnp.int32),
                 pltpu.VMEM((16, D), BF16),
                 pltpu.VMEM((32, 128), BF16),
                 pltpu.VMEM((32, 128), BF16),
@@ -492,11 +555,15 @@
                 dma((2, NR)),
                 dma((2, 4, NR)),
                 dma((2, 4, NR)),
+                dma((2, 4, len(HAND))),
+                dma((2, 4, len(HAND))),
+                dma((2, 4, len(HAND))),
+                dma((2, 4, len(HAND))),
             ],
             compiler_params=pltpu.CompilerParams(collective_id=0, has_side_effects=True, vmem_limit_bytes=VMEM_LIMIT),
             name="layer",
         )(
-            jnp.broadcast_to(start_pos[:, None], (8, 128)), x_in.reshape(16, D), freq, kc2, vc2, attn_gain.reshape(32, 128), w_query.reshape(4 * D, 128),
+            start_pos, x_in.reshape(16, D), freq, kc2, vc2, attn_gain.reshape(32, 128), w_query.reshape(4 * D, 128),
             w_key.reshape(D, 128), w_value.reshape(D, 128), w_out.reshape(512, D), mlp_gain.reshape(32, 128), w_gate, w_up, w_down,
         )
         x_out, k_new, v_new = pl.pallas_call(

time: 52.7 us -> 53.1 us (level)
  Pallas kernels: 50.5 us -> 51.5 us
  local copies, waits for them, and re-layouts: 0.59 us -> 0 us
    pallas_call x1, Pallas kernels: 49.2 us -> 50.2 us  [local_layer(): pl.pallas_call(layer_kernel, out_shape=(pltpu.VMEM((16, D), BF16), pltpu....]
    broadcast_in_dim x1 -> x0, local copies, waits for them, and re-layouts: 0.59 us -> none  [local_layer(): jnp.broadcast_to(start_pos[:, None], (8, 128))]
where the time goes in v7:
time: 53.1 us; the launch traced here: 53 us
  Pallas kernels  51.5 us (97%)
  between operations  1.45 us (3%)
    pallas_call x1, Pallas kernels, local_layer(): pl.pallas_call(layer_kernel, out_shape=(pltpu.VMEM((16, D), BF16), pltpu....  50.2 us
    pallas_call x1, Pallas kernels, local_layer(): pl.pallas_call(write_kernel, out_shape=(jax.ShapeDtypeStruct((16, D), BF1...  1.37 us

profile of v7, /device:TPU:0, one launch (start us, length us, event | category | flops | bytes accessed | tf_op | source)
XLA Modules:
  0.0 53.0 jit_solution(12539490716896464855)
XLA Ops:
  1.3 50.2 %layer.1 = (bf16[16,4096]{1,0:T(8,128)(2,1)S(1)}, bf16[4096,128]{1,0:T(8,128)(2,1)S(1)}, bf16[4096,128]{1,0:T(8,128)(2,1)S(1)}) custom-call(s32[1]{0:T(128)S(6)} %copy.17.start_hbm, bf16[16,4096]{1,0:T(8,128)(2,1)} %bitcast.18, f32[8,128]{1,0:T(8,128)} %constant.2.clone.freq_hbm, bf16[4096,128]{1,0:T(8,128)(2,1)} %bitcast.14, bf16[4096,128]{1,0:T(8,128)(2,1)} %bitcast.15, ...), custom_call_target="tpu_custom_call" | custom-call | tf_op jit(solution)/shard_map/layer/pallas_call | solution.py:527
  51.4 1.4 %write.1 = (bf16[16,4096]{1,0:T(8,128)(2,1)}, bf16[4096,128]{1,0:T(8,128)(2,1)}, bf16[4096,128]{1,0:T(8,128)(2,1)}) custom-call(bf16[16,4096]{1,0:T(8,128)(2,1)S(1)} %get-tuple-element.9.x_ref, bf16[4096,128]{1,0:T(8,128)(2,1)S(1)} %get-tuple-element.10.k_ref, bf16[4096,128]{1,0:T(8,128)(2,1)S(1)} %get-tuple-element.11.v_ref), custom_call_target="tpu_custom_call" | custom-call | tf_op jit(solution)/shard_map/write/pallas_call | solution.py:569

commit v8 on v6

--- a/solution.py
+++ b/solution.py
@@ -21,9 +21,10 @@
 GATHER = [(512 * p, 512) for p in range(7)] + [(3584, 256), (3840, 256)]
 SCATTER = [(512 * p, 512) for p in range(8)]
 NA = len(GATHER)
+NW = 4
 NR = len(SCATTER)
 LAG = 2
-VIA = 4
+VIA = 6
 VMEM_LIMIT = 64000000
 KB = 512
 NKB = W // KB
@@ -38,7 +39,7 @@
 def layer_kernel(start_hbm, x_hbm, freq_hbm, kc_hbm, vc_hbm, g1_hbm, wq_hbm, wk_hbm, wv_hbm, wo_hbm, g2_hbm, wg_hbm, wu_hbm, wd_hbm,
                  xo_ref, kn_ref, vn_ref,
                  start_ref, xv, g1, g2, wg, wu, xg1, xg2, pbuf, ra, sb, rb, tb, hb,
-                 lsem, wsem, dsem, send_sem, recv_sem, fsend_sem, frecv_sem, asend_sem, arecv_sem, bsend_sem, brecv_sem):
+                 lsem, wsem, dsem, gsend_sem, drecv_sem, frecv_sem, asend_sem, arecv_sem, bsend_sem, brecv_sem, trecv_sem):
     me = lax.axis_index("tp")
     core = me % 2
     chip = me // 2
@@ -59,21 +60,16 @@
     def local(src, dst, sem):
         return pltpu.make_async_copy(src, dst, sem)
 
+    def piece(xg, c, r, p):
+        return xg.at[rows_of(c, chips[r]), pl.ds(*GATHER[p])]
+
     def ag_direct(ph, xg, r, p):
-        cols = pl.ds(*GATHER[p])
-        return remote(xg.at[my_rows, cols], xg.at[my_rows, cols], send_sem.at[ph, r, p], recv_sem.at[ph, r, p], 2 * chips[r] + core)
-
-    def ag_direct_in(ph, xg, r, p):
-        ref = xg.at[rows_of(core, chips[r]), pl.ds(*GATHER[p])]
-        return remote(ref, ref, send_sem.at[ph, r, p], recv_sem.at[ph, r, p], 2 * chips[r] + core)
+        ref = piece(xg, core, 0, p)
+        return remote(ref, ref, gsend_sem.at[ph], drecv_sem.at[ph, p], 2 * chips[r] + core)
 
     def ag_forward(ph, xg, r, p):
-        ref = xg.at[rows_of(core, chips[r]), pl.ds(*GATHER[p])]
-        return remote(ref, ref, fsend_sem.at[ph, r, p], frecv_sem.at[ph, r, p], partner)
-
-    def ag_forward_in(ph, xg, r, p):
-        ref = xg.at[rows_of(other, chips[r]), pl.ds(*GATHER[p])]
-        return remote(ref, ref, fsend_sem.at[ph, r, p], frecv_sem.at[ph, r, p], partner)
+        ref = piece(xg, core, r, p)
+        return remote(ref, ref, gsend_sem.at[ph], frecv_sem.at[ph, p], partner)
 
     def ag_start(ph, xg):
         for p in range(NA):
@@ -82,28 +78,26 @@
             ag_forward(ph, xg, 0, p).start()
 
     def ag_relay(ph, xg, p):
+        ref = xg.at[pl.ds(0, 48), pl.ds(*GATHER[p])]
+        remote(ref, ref, gsend_sem.at[ph], drecv_sem.at[ph, p], partner).wait_recv()
         for r in (1, 2, 3):
-            ag_direct_in(ph, xg, r, p).wait_recv()
             ag_forward(ph, xg, r, p).start()
 
     def ag_arrive(ph, xg, p):
-        for r in (0, 1, 2, 3):
-            ag_forward_in(ph, xg, r, p).wait_recv()
+        ref = xg.at[pl.ds(0, 64), pl.ds(*GATHER[p])]
+        remote(ref, ref, gsend_sem.at[ph], frecv_sem.at[ph, p], partner).wait_recv()
 
     def ag_finish(ph, xg):
-        for p in range(NA):
-            for r in (1, 2, 3):
-                ag_direct(ph, xg, r, p).wait_send()
-            for r in (0, 1, 2, 3):
-                ag_forward(ph, xg, r, p).wait_send()
+        ref = xg.at[pl.ds(0, 112), :]
+        remote(ref, ref, gsend_sem.at[ph], drecv_sem.at[ph, 0], partner).wait_send()
 
     def rs_a(ph, n):
         cols = pl.ds(*SCATTER[n])
-        return remote(pbuf.at[ph, pl.ds(pl.multiple_of(64 * other, 64), 64), cols], ra.at[ph, :, cols], asend_sem.at[ph, n], arecv_sem.at[ph, n], partner)
+        return remote(pbuf.at[ph, pl.ds(pl.multiple_of(64 * other, 64), 64), cols], ra.at[ph, :, cols], asend_sem.at[ph], arecv_sem.at[ph, n], partner)
 
     def rs_b(ph, n, r):
         cols = pl.ds(*SCATTER[n])
-        return remote(sb.at[ph, pl.ds(pl.multiple_of(16 * chips[r], 16), 16), cols], rb.at[ph, r - 1, :, cols], bsend_sem.at[ph, r, n], brecv_sem.at[ph, r, n], 2 * chips[r] + core)
+        return remote(sb.at[ph, pl.ds(pl.multiple_of(16 * chips[r], 16), 16), cols], rb.at[ph, r - 1, :, cols], bsend_sem.at[ph], brecv_sem.at[ph, n], 2 * chips[r] + core)
 
     def rs_put(ph, n, part):
         pbuf[ph, :, pl.ds(*SCATTER[n])] = part.astype(BF16)
@@ -115,7 +109,7 @@
     def rs_transit(ph, n):
         cols = pl.ds(*SCATTER[n])
         src = sb.at[ph, pl.ds(pl.multiple_of(16 * chips[3], 16), 16), cols]
-        return remote(src, tb.at[ph, :, cols], bsend_sem.at[ph, 3, n], brecv_sem.at[ph, 3, n], 2 * chips[rs_first(n)] + core)
+        return remote(src, tb.at[ph, :, cols], bsend_sem.at[ph], trecv_sem.at[ph, n], 2 * chips[rs_first(n)] + core)
 
     def rs_pair(ph, n):
         cols = pl.ds(*SCATTER[n])
@@ -153,17 +147,16 @@
     def rs_sum(ph, n):
         cols = pl.ds(*SCATTER[n])
         total = sb[ph, pl.ds(pl.multiple_of(16 * chip, 16), 16), cols].astype(F32)
-        for r in (1, 2) if n < VIA else (1, 2, 3):
-            rs_b(ph, n, r).wait_recv()
+        count = 2 if n < VIA else 3
+        ref = rb.at[ph, pl.ds(0, count), :, cols]
+        remote(ref, ref, bsend_sem.at[ph], brecv_sem.at[ph, n], partner).wait_recv()
+        for r in range(1, count + 1):
             total = total + rb[ph, r - 1, :, cols].astype(F32)
         return total
 
     def rs_finish(ph):
-        for n in range(NR):
-            rs_a(ph, n).wait_send()
-            for r in (1, 2):
-                rs_b(ph, n, r).wait_send()
-            (rs_transit(ph, n) if n < VIA else rs_b(ph, n, 3)).wait_send()
+        remote(ra.at[ph], ra.at[ph], asend_sem.at[ph], arecv_sem.at[ph, 0], partner).wait_send()
+        remote(rb.at[ph], rb.at[ph], bsend_sem.at[ph], brecv_sem.at[ph, 0], partner).wait_send()
 
     def normed(rows, gain):
         ms = jnp.zeros((16, 128), F32)
@@ -180,11 +173,7 @@
             val = src[:, cols].astype(F32) * inv * gain[j:j + 1, :].astype(F32)
             dst[my_rows, cols] = val.astype(BF16)
 
-    gate_loads = []
-    for p in range(NA):
-        rows = pl.ds(*GATHER[p])
-        gate_loads.append(local(wg_hbm.at[rows, :], wg.at[rows, :], wsem.at[0, p]))
-        gate_loads.append(local(wu_hbm.at[rows, :], wu.at[rows, :], wsem.at[1, p]))
+    gate_loads = [local(wg_hbm, wg, wsem.at[0]), local(wu_hbm, wu, wsem.at[1])]
 
     def attention_phase(kc, vc, vt, wo, freqv, qt, kch, vch, bias, o_buf):
         loads = {
@@ -207,7 +196,7 @@
         def projection_phase(wq4, wqkv):
             wk_load = local(wk_hbm, wqkv.at[:, pl.ds(512, 128)], lsem.at[2])
             wv_load = local(wv_hbm, wqkv.at[:, pl.ds(640, 128)], lsem.at[3])
-            wq_loads = [local(wq_hbm.at[pl.ds(p * 4 * CW, 4 * CW), :], wq4.at[pl.ds(p * 4 * CW, 4 * CW), :], dsem.at[p]) for p in range(NP)]
+            wq_loads = [local(wq_hbm.at[pl.ds(p * 4 * (D // NW), 4 * (D // NW)), :], wq4.at[pl.ds(p * 4 * (D // NW), 4 * (D // NW)), :], dsem.at[p]) for p in range(NW)]
             for ld in wq_loads:
                 ld.start()
             loads["vc"].start()
@@ -229,7 +218,8 @@
             perm = (ci == 4 * (ri % 64) + ri // 64).astype(F32).astype(BF16)
 
             def split_heads(p):
-                wq_loads[p].wait()
+                if p % (NP // NW) == 0:
+                    wq_loads[p // (NP // NW)].wait()
 
                 def body(i, carry):
                     base = p * (CW // 64) + 2 * i
@@ -255,7 +245,7 @@
                 return carry
 
             loads["start"].wait()
-            start = start_ref[0:1, :]
+            start = start_ref[0]
             for p in range(4):
                 split_heads(p)
             for p in range(6):
@@ -369,7 +359,7 @@
             vn_ref[ks, :] = jnp.where(fresh, placed[:, 128:256], vc[ks, :].astype(F32)).astype(BF16)
             return carry
 
-        start = start_ref[0:1, :]
+        start = start_ref[0]
         lax.fori_loop(0, NKB, merge, 0)
 
     pl.run_scoped(
@@ -387,9 +377,8 @@
     )
 
     def mlp_phase(wd, acc_g, acc_u, u_buf):
-        down_loads = [local(wd_hbm.at[:, pl.ds(n * CW, CW)], wd.at[:, pl.ds(n * CW, CW)], dsem.at[n]) for n in range(NP)]
-        for ld in down_loads:
-            ld.start()
+        down_load = local(wd_hbm, wd, wsem.at[2])
+        down_load.start()
         for n in range(NR):
             cols = pl.ds(*SCATTER[n])
             hb[:, cols] = (xv[:, cols].astype(F32) + rs_sum(0, n)).astype(BF16)
@@ -402,8 +391,9 @@
         for p in range(NA):
             if p + 2 < NA:
                 ag_relay(1, xg2, p + 2)
-            gate_loads[2 * p].wait()
-            gate_loads[2 * p + 1].wait()
+            if p == 0:
+                for ld in gate_loads:
+                    ld.wait()
             ag_arrive(1, xg2, p)
             rows = pl.ds(*GATHER[p])
             m = xg2[:, rows]
@@ -419,7 +409,8 @@
                 gate = acc_g[...] + gate
                 u_buf[...] = (gate / (1.0 + jnp.exp(-gate)) * (acc_u[...] + up)).astype(BF16)
         def down(n, cols):
-            down_loads[n].wait()
+            if n == 0:
+                down_load.wait()
             return jnp.dot(u_buf[...], wd[:, cols], preferred_element_type=F32)
 
         rs_all(1, down, 1)
@@ -467,7 +458,7 @@
             in_specs=[any_spec] * 14,
             out_specs=(vmem_spec, vmem_spec, vmem_spec),
             scratch_shapes=[
-                pltpu.VMEM((8, 128), jnp.int32),
+                pltpu.SMEM((1,), jnp.int32),
                 pltpu.VMEM((16, D), BF16),
                 pltpu.VMEM((32, 128), BF16),
                 pltpu.VMEM((32, 128), BF16),
@@ -482,21 +473,21 @@
                 pltpu.VMEM((2, 16, VIA * CW), BF16),
                 pltpu.VMEM((16, D), BF16),
                 dma((10,)),
+                dma((3,)),
+                dma((NW,)),
+                dma((2,)),
                 dma((2, NA)),
-                dma((NP,)),
-                dma((2, 4, NA)),
-                dma((2, 4, NA)),
-                dma((2, 4, NA)),
-                dma((2, 4, NA)),
+                dma((2, NA)),
+                dma((2,)),
                 dma((2, NR)),
+                dma((2,)),
                 dma((2, NR)),
-                dma((2, 4, NR)),
-                dma((2, 4, NR)),
+                dma((2, VIA)),
             ],
             compiler_params=pltpu.CompilerParams(collective_id=0, has_side_effects=True, vmem_limit_bytes=VMEM_LIMIT),
             name="layer",
         )(
-            jnp.broadcast_to(start_pos[:, None], (8, 128)), x_in.reshape(16, D), freq, kc2, vc2, attn_gain.reshape(32, 128), w_query.reshape(4 * D, 128),
+            start_pos, x_in.reshape(16, D), freq, kc2, vc2, attn_gain.reshape(32, 128), w_query.reshape(4 * D, 128),
             w_key.reshape(D, 128), w_value.reshape(D, 128), w_out.reshape(512, D), mlp_gain.reshape(32, 128), w_gate, w_up, w_down,
         )
         x_out, k_new, v_new = pl.pallas_call(

time: 52.7 us -> 48.3 us (0.917)
  Pallas kernels: 50.5 us -> 46.8 us
  local copies, waits for them, and re-layouts: 0.59 us -> 0 us
    pallas_call x1, Pallas kernels: 49.2 us -> 45.4 us  [local_layer(): pl.pallas_call(layer_kernel, out_shape=(pltpu.VMEM((16, D), BF16), pltpu....]
    broadcast_in_dim x1 -> x0, local copies, waits for them, and re-layouts: 0.59 us -> none  [local_layer(): jnp.broadcast_to(start_pos[:, None], (8, 128))]
where the time goes in v8:
time: 48.3 us; the launch traced here: 48.2 us
  Pallas kernels  46.8 us (97%)
  between operations  1.45 us (3%)
    pallas_call x1, Pallas kernels, local_layer(): pl.pallas_call(layer_kernel, out_shape=(pltpu.VMEM((16, D), BF16), pltpu....  45.4 us
    pallas_call x1, Pallas kernels, local_layer(): pl.pallas_call(write_kernel, out_shape=(jax.ShapeDtypeStruct((16, D), BF1...  1.37 us

profile of v8, /device:TPU:0, one launch (start us, length us, event | category | flops | bytes accessed | tf_op | source)
XLA Modules:
  0.0 48.2 jit_solution(14473953986668074936)
XLA Ops:
  1.3 45.4 %layer.1 = (bf16[16,4096]{1,0:T(8,128)(2,1)S(1)}, bf16[4096,128]{1,0:T(8,128)(2,1)S(1)}, bf16[4096,128]{1,0:T(8,128)(2,1)S(1)}) custom-call(s32[1]{0:T(128)S(6)} %copy.17.start_hbm, bf16[16,4096]{1,0:T(8,128)(2,1)} %bitcast.18, f32[8,128]{1,0:T(8,128)} %constant.2.clone.freq_hbm, bf16[4096,128]{1,0:T(8,128)(2,1)} %bitcast.14, bf16[4096,128]{1,0:T(8,128)(2,1)} %bitcast.15, ...), custom_call_target="tpu_custom_call" | custom-call | tf_op jit(solution)/shard_map/layer/pallas_call | solution.py:455
  46.7 1.4 %write.1 = (bf16[16,4096]{1,0:T(8,128)(2,1)}, bf16[4096,128]{1,0:T(8,128)(2,1)}, bf16[4096,128]{1,0:T(8,128)(2,1)}) custom-call(bf16[16,4096]{1,0:T(8,128)(2,1)S(1)} %get-tuple-element.9.x_ref, bf16[4096,128]{1,0:T(8,128)(2,1)S(1)} %get-tuple-element.10.k_ref, bf16[4096,128]{1,0:T(8,128)(2,1)S(1)} %get-tuple-element.11.v_ref), custom_call_target="tpu_custom_call" | custom-call | tf_op jit(solution)/shard_map/write/pallas_call | solution.py:493

commit v9 on v8

--- a/solution.py
+++ b/solution.py
@@ -18,10 +18,10 @@
 W = 4096
 NP = 8
 CW = D // NP
-GATHER = [(512 * p, 512) for p in range(7)] + [(3584, 256), (3840, 256)]
+GATHER = [(0, 256), (256, 256)] + [(512 * p, 512) for p in range(1, 7)] + [(3584, 256), (3840, 256)]
 SCATTER = [(512 * p, 512) for p in range(8)]
 NA = len(GATHER)
-NW = 4
+NW = 2
 NR = len(SCATTER)
 LAG = 2
 VIA = 6
@@ -65,11 +65,11 @@
 
     def ag_direct(ph, xg, r, p):
         ref = piece(xg, core, 0, p)
-        return remote(ref, ref, gsend_sem.at[ph], drecv_sem.at[ph, p], 2 * chips[r] + core)
+        return remote(ref, ref, gsend_sem.at[ph], drecv_sem.at[p], 2 * chips[r] + core)
 
     def ag_forward(ph, xg, r, p):
         ref = piece(xg, core, r, p)
-        return remote(ref, ref, gsend_sem.at[ph], frecv_sem.at[ph, p], partner)
+        return remote(ref, ref, gsend_sem.at[ph], frecv_sem.at[p], partner)
 
     def ag_start(ph, xg):
         for p in range(NA):
@@ -79,25 +79,25 @@
 
     def ag_relay(ph, xg, p):
         ref = xg.at[pl.ds(0, 48), pl.ds(*GATHER[p])]
-        remote(ref, ref, gsend_sem.at[ph], drecv_sem.at[ph, p], partner).wait_recv()
+        remote(ref, ref, gsend_sem.at[ph], drecv_sem.at[p], partner).wait_recv()
         for r in (1, 2, 3):
             ag_forward(ph, xg, r, p).start()
 
     def ag_arrive(ph, xg, p):
         ref = xg.at[pl.ds(0, 64), pl.ds(*GATHER[p])]
-        remote(ref, ref, gsend_sem.at[ph], frecv_sem.at[ph, p], partner).wait_recv()
+        remote(ref, ref, gsend_sem.at[ph], frecv_sem.at[p], partner).wait_recv()
 
     def ag_finish(ph, xg):
         ref = xg.at[pl.ds(0, 112), :]
-        remote(ref, ref, gsend_sem.at[ph], drecv_sem.at[ph, 0], partner).wait_send()
+        remote(ref, ref, gsend_sem.at[ph], drecv_sem.at[0], partner).wait_send()
 
     def rs_a(ph, n):
         cols = pl.ds(*SCATTER[n])
-        return remote(pbuf.at[ph, pl.ds(pl.multiple_of(64 * other, 64), 64), cols], ra.at[ph, :, cols], asend_sem.at[ph], arecv_sem.at[ph, n], partner)
+        return remote(pbuf.at[ph, pl.ds(pl.multiple_of(64 * other, 64), 64), cols], ra.at[ph, :, cols], asend_sem.at[ph], arecv_sem.at[n], partner)
 
     def rs_b(ph, n, r):
         cols = pl.ds(*SCATTER[n])
-        return remote(sb.at[ph, pl.ds(pl.multiple_of(16 * chips[r], 16), 16), cols], rb.at[ph, r - 1, :, cols], bsend_sem.at[ph], brecv_sem.at[ph, n], 2 * chips[r] + core)
+        return remote(sb.at[ph, pl.ds(pl.multiple_of(16 * chips[r], 16), 16), cols], rb.at[ph, r - 1, :, cols], bsend_sem.at[ph], brecv_sem.at[n], 2 * chips[r] + core)
 
     def rs_put(ph, n, part):
         pbuf[ph, :, pl.ds(*SCATTER[n])] = part.astype(BF16)
@@ -109,7 +109,7 @@
     def rs_transit(ph, n):
         cols = pl.ds(*SCATTER[n])
         src = sb.at[ph, pl.ds(pl.multiple_of(16 * chips[3], 16), 16), cols]
-        return remote(src, tb.at[ph, :, cols], bsend_sem.at[ph], trecv_sem.at[ph, n], 2 * chips[rs_first(n)] + core)
+        return remote(src, tb.at[ph, :, cols], bsend_sem.at[ph], trecv_sem.at[n], 2 * chips[rs_first(n)] + core)
 
     def rs_pair(ph, n):
         cols = pl.ds(*SCATTER[n])
@@ -149,14 +149,14 @@
         total = sb[ph, pl.ds(pl.multiple_of(16 * chip, 16), 16), cols].astype(F32)
         count = 2 if n < VIA else 3
         ref = rb.at[ph, pl.ds(0, count), :, cols]
-        remote(ref, ref, bsend_sem.at[ph], brecv_sem.at[ph, n], partner).wait_recv()
+        remote(ref, ref, bsend_sem.at[ph], brecv_sem.at[n], partner).wait_recv()
         for r in range(1, count + 1):
             total = total + rb[ph, r - 1, :, cols].astype(F32)
         return total
 
     def rs_finish(ph):
-        remote(ra.at[ph], ra.at[ph], asend_sem.at[ph], arecv_sem.at[ph, 0], partner).wait_send()
-        remote(rb.at[ph], rb.at[ph], bsend_sem.at[ph], brecv_sem.at[ph, 0], partner).wait_send()
+        remote(ra.at[ph], ra.at[ph], asend_sem.at[ph], arecv_sem.at[0], partner).wait_send()
+        remote(rb.at[ph], rb.at[ph], bsend_sem.at[ph], brecv_sem.at[0], partner).wait_send()
 
     def normed(rows, gain):
         ms = jnp.zeros((16, 128), F32)
@@ -476,13 +476,13 @@
                 dma((3,)),
                 dma((NW,)),
                 dma((2,)),
-                dma((2, NA)),
-                dma((2, NA)),
+                dma((NA,)),
+                dma((NA,)),
                 dma((2,)),
-                dma((2, NR)),
+                dma((NR,)),
                 dma((2,)),
-                dma((2, NR)),
-                dma((2, VIA)),
+                dma((NR,)),
+                dma((VIA,)),
             ],
             compiler_params=pltpu.CompilerParams(collective_id=0, has_side_effects=True, vmem_limit_bytes=VMEM_LIMIT),
             name="layer",

time: 48.3 us -> 48 us (level)
  no operation moved by 1% of the time
where the time goes in v9:
time: 48 us; the launch traced here: 47.9 us
  Pallas kernels  46.4 us (97%)
  between operations  1.45 us (3%)
    pallas_call x1, Pallas kernels, local_layer(): pl.pallas_call(layer_kernel, out_shape=(pltpu.VMEM((16, D), BF16), pltpu....  45.1 us
    pallas_call x1, Pallas kernels, local_layer(): pl.pallas_call(write_kernel, out_shape=(jax.ShapeDtypeStruct((16, D), BF1...  1.37 us

profile of v9, /device:TPU:0, one launch (start us, length us, event | category | flops | bytes accessed | tf_op | source)
XLA Modules:
  0.0 47.9 jit_solution(3583559735904394177)
XLA Ops:
  1.3 45.1 %layer.1 = (bf16[16,4096]{1,0:T(8,128)(2,1)S(1)}, bf16[4096,128]{1,0:T(8,128)(2,1)S(1)}, bf16[4096,128]{1,0:T(8,128)(2,1)S(1)}) custom-call(s32[1]{0:T(128)S(6)} %copy.17.start_hbm, bf16[16,4096]{1,0:T(8,128)(2,1)} %bitcast.18, f32[8,128]{1,0:T(8,128)} %constant.2.clone.freq_hbm, bf16[4096,128]{1,0:T(8,128)(2,1)} %bitcast.14, bf16[4096,128]{1,0:T(8,128)(2,1)} %bitcast.15, ...), custom_call_target="tpu_custom_call" | custom-call | tf_op jit(solution)/shard_map/layer/pallas_call | solution.py:455
  46.3 1.4 %write.1 = (bf16[16,4096]{1,0:T(8,128)(2,1)}, bf16[4096,128]{1,0:T(8,128)(2,1)}, bf16[4096,128]{1,0:T(8,128)(2,1)}) custom-call(bf16[16,4096]{1,0:T(8,128)(2,1)S(1)} %get-tuple-element.9.x_ref, bf16[4096,128]{1,0:T(8,128)(2,1)S(1)} %get-tuple-element.10.k_ref, bf16[4096,128]{1,0:T(8,128)(2,1)S(1)} %get-tuple-element.11.v_ref), custom_call_target="tpu_custom_call" | custom-call | tf_op jit(solution)/shard_map/write/pallas_call | solution.py:493

commit v10 on v9

--- a/solution.py
+++ b/solution.py
@@ -270,11 +270,14 @@
                     split_heads(p + 4)
                 if p < 2:
                     flip_values(p + 6, 0)
+                if p == NA - 2:
+                    for name in ("kc", "wo", "g2"):
+                        loads[name].wait()
+                    for ld in gate_loads:
+                        ld.start()
                 ag_arrive(0, xg1, p)
                 cols = pl.ds(*GATHER[p])
                 acc = acc + jnp.dot(xg1[:, cols], wqkv[cols, :], preferred_element_type=F32)
-            for ld in gate_loads:
-                ld.start()
 
             def rotate(v):
                 swapped = jnp.where(even, pltpu.roll(v, 127, 1), pltpu.roll(v, 1, 1))
@@ -292,7 +295,6 @@
             pltpu.VMEM((4 * D, 128), BF16),
             pltpu.VMEM((D, 768), BF16),
         )
-        loads["kc"].wait()
         factor = (128.0 ** -0.5) * 1.4426950408889634
 
         def softmax_phase(e_buf):
@@ -342,9 +344,7 @@
                 o_buf[:, g * 128:g * 128 + 128] = out[:, g * 128:g * 128 + 128].T.astype(BF16)
 
         pl.run_scoped(softmax_phase, pltpu.VMEM((W + T, 512), F32))
-        loads["wo"].wait()
         rs_all(0, lambda n, cols: jnp.dot(o_buf[...], wo[:, cols], preferred_element_type=F32), 2)
-        loads["g2"].wait()
 
         chunk = jnp.concatenate([kch[...], vch[...]], axis=1)
 
@@ -430,7 +430,11 @@
 
 
 def write_kernel(x_ref, k_ref, v_ref, xo_hbm, ko_hbm, vo_hbm, sem):
-    copies = [pltpu.make_async_copy(src, dst, sem.at[i]) for i, (src, dst) in enumerate(((k_ref, ko_hbm), (v_ref, vo_hbm), (x_ref, xo_hbm)))]
+    parts = [(x_ref, xo_hbm)]
+    for i in range(4):
+        rows = pl.ds(i * (W // 4), W // 4)
+        parts += [(k_ref.at[rows, :], ko_hbm.at[rows, :]), (v_ref.at[rows, :], vo_hbm.at[rows, :])]
+    copies = [pltpu.make_async_copy(src, dst, sem.at[i]) for i, (src, dst) in enumerate(parts)]
     for copy in copies:
         copy.start()
     for copy in copies:
@@ -495,7 +499,7 @@
             out_shape=(jax.ShapeDtypeStruct((16, D), BF16), jax.ShapeDtypeStruct((W, 128), BF16), jax.ShapeDtypeStruct((W, 128), BF16)),
             in_specs=[vmem_spec] * 3,
             out_specs=(pl.BlockSpec(memory_space=pltpu.HBM),) * 3,
-            scratch_shapes=[dma((3,))],
+            scratch_shapes=[dma((9,))],
             compiler_params=pltpu.CompilerParams(vmem_limit_bytes=1 << 20),
             name="write",
         )(*[pltpu.with_memory_space_constraint(r, pltpu.VMEM) for r in results])

time: 48 us -> 48 us (level)
  no operation moved by 1% of the time
where the time goes in v10:
time: 48 us; the launch traced here: 47.9 us
  Pallas kernels  46.5 us (97%)
  between operations  1.45 us (3%)
    pallas_call x1, Pallas kernels, local_layer(): pl.pallas_call(layer_kernel, out_shape=(pltpu.VMEM((16, D), BF16), pltpu....  45 us
    pallas_call x1, Pallas kernels, local_layer(): pl.pallas_call(write_kernel, out_shape=(jax.ShapeDtypeStruct((16, D), BF1...  1.43 us

profile of v10, /device:TPU:0, one launch (start us, length us, event | category | flops | bytes accessed | tf_op | source)
XLA Modules:
  0.0 47.9 jit_solution(11003057467022582763)
XLA Ops:
  1.3 45.0 %layer.1 = (bf16[16,4096]{1,0:T(8,128)(2,1)S(1)}, bf16[4096,128]{1,0:T(8,128)(2,1)S(1)}, bf16[4096,128]{1,0:T(8,128)(2,1)S(1)}) custom-call(s32[1]{0:T(128)S(6)} %copy.17.start_hbm, bf16[16,4096]{1,0:T(8,128)(2,1)} %bitcast.18, f32[8,128]{1,0:T(8,128)} %constant.2.clone.freq_hbm, bf16[4096,128]{1,0:T(8,128)(2,1)} %bitcast.14, bf16[4096,128]{1,0:T(8,128)(2,1)} %bitcast.15, ...), custom_call_target="tpu_custom_call" | custom-call | tf_op jit(solution)/shard_map/layer/pallas_call | solution.py:459
  46.3 1.4 %write.1 = (bf16[16,4096]{1,0:T(8,128)(2,1)}, bf16[4096,128]{1,0:T(8,128)(2,1)}, bf16[4096,128]{1,0:T(8,128)(2,1)}) custom-call(bf16[16,4096]{1,0:T(8,128)(2,1)S(1)} %get-tuple-element.9.x_ref, bf16[4096,128]{1,0:T(8,128)(2,1)S(1)} %get-tuple-element.10.k_ref, bf16[4096,128]{1,0:T(8,128)(2,1)S(1)} %get-tuple-element.11.v_ref), custom_call_target="tpu_custom_call" | custom-call | tf_op jit(solution)/shard_map/write/pallas_call | solution.py:497

commit v11 on v10

--- a/solution.py
+++ b/solution.py
@@ -394,6 +394,8 @@
             if p == 0:
                 for ld in gate_loads:
                     ld.wait()
+            if p == NA - 2:
+                down_load.wait()
             ag_arrive(1, xg2, p)
             rows = pl.ds(*GATHER[p])
             m = xg2[:, rows]
@@ -409,8 +411,6 @@
                 gate = acc_g[...] + gate
                 u_buf[...] = (gate / (1.0 + jnp.exp(-gate)) * (acc_u[...] + up)).astype(BF16)
         def down(n, cols):
-            if n == 0:
-                down_load.wait()
             return jnp.dot(u_buf[...], wd[:, cols], preferred_element_type=F32)
 
         rs_all(1, down, 1)
@@ -430,11 +430,7 @@
 
 
 def write_kernel(x_ref, k_ref, v_ref, xo_hbm, ko_hbm, vo_hbm, sem):
-    parts = [(x_ref, xo_hbm)]
-    for i in range(4):
-        rows = pl.ds(i * (W // 4), W // 4)
-        parts += [(k_ref.at[rows, :], ko_hbm.at[rows, :]), (v_ref.at[rows, :], vo_hbm.at[rows, :])]
-    copies = [pltpu.make_async_copy(src, dst, sem.at[i]) for i, (src, dst) in enumerate(parts)]
+    copies = [pltpu.make_async_copy(src, dst, sem.at[i]) for i, (src, dst) in enumerate(((k_ref, ko_hbm), (v_ref, vo_hbm), (x_ref, xo_hbm)))]
     for copy in copies:
         copy.start()
     for copy in copies:
@@ -499,7 +495,7 @@
             out_shape=(jax.ShapeDtypeStruct((16, D), BF16), jax.ShapeDtypeStruct((W, 128), BF16), jax.ShapeDtypeStruct((W, 128), BF16)),
             in_specs=[vmem_spec] * 3,
             out_specs=(pl.BlockSpec(memory_space=pltpu.HBM),) * 3,
-            scratch_shapes=[dma((9,))],
+            scratch_shapes=[dma((3,))],
             compiler_params=pltpu.CompilerParams(vmem_limit_bytes=1 << 20),
             name="write",
         )(*[pltpu.with_memory_space_constraint(r, pltpu.VMEM) for r in results])

time: 48 us -> 47.8 us (level)
  no operation moved by 1% of the time
where the time goes in v11:
time: 47.8 us; the launch traced here: 47.7 us
  Pallas kernels  46.2 us (97%)
  between operations  1.45 us (3%)
    pallas_call x1, Pallas kernels, local_layer(): pl.pallas_call(layer_kernel, out_shape=(pltpu.VMEM((16, D), BF16), pltpu....  44.9 us
    pallas_call x1, Pallas kernels, local_layer(): pl.pallas_call(write_kernel, out_shape=(jax.ShapeDtypeStruct((16, D), BF1...  1.37 us

profile of v11, /device:TPU:0, one launch (start us, length us, event | category | flops | bytes accessed | tf_op | source)
XLA Modules:
  0.0 47.7 jit_solution(15229963410503529180)
XLA Ops:
  1.3 44.9 %layer.1 = (bf16[16,4096]{1,0:T(8,128)(2,1)S(1)}, bf16[4096,128]{1,0:T(8,128)(2,1)S(1)}, bf16[4096,128]{1,0:T(8,128)(2,1)S(1)}) custom-call(s32[1]{0:T(128)S(6)} %copy.17.start_hbm, bf16[16,4096]{1,0:T(8,128)(2,1)} %bitcast.18, f32[8,128]{1,0:T(8,128)} %constant.2.clone.freq_hbm, bf16[4096,128]{1,0:T(8,128)(2,1)} %bitcast.14, bf16[4096,128]{1,0:T(8,128)(2,1)} %bitcast.15, ...), custom_call_target="tpu_custom_call" | custom-call | tf_op jit(solution)/shard_map/layer/pallas_call | solution.py:455
  46.2 1.4 %write.1 = (bf16[16,4096]{1,0:T(8,128)(2,1)}, bf16[4096,128]{1,0:T(8,128)(2,1)}, bf16[4096,128]{1,0:T(8,128)(2,1)}) custom-call(bf16[16,4096]{1,0:T(8,128)(2,1)S(1)} %get-tuple-element.9.x_ref, bf16[4096,128]{1,0:T(8,128)(2,1)S(1)} %get-tuple-element.10.k_ref, bf16[4096,128]{1,0:T(8,128)(2,1)S(1)} %get-tuple-element.11.v_ref), custom_call_target="tpu_custom_call" | custom-call | tf_op jit(solution)/shard_map/write/pallas_call | solution.py:493
